TPU v7x, 512 devices: a whole 4x8x8 slice. The times are simulated.
512 devices in a mesh: lat: 64 (over x, z, core), chan: 8 (over y).
Axes of the slice: x: 4, y: 8, z: 8, core: 2. Of those that a mesh axis runs over, the one named last changes fastest.
Arguments:
- spec_in: bfloat16 [384, 1, 256, 2, 384], P('lat', None, 'chan'), may hold values from -6 to 6
- legendre: float32 [384, 384, 384], P('lat'), may hold values from -0.4375 to 0.4375
- mode_slot: int32 [384], replicated, may hold values from 0 to 383, each once
- w_in: bfloat16 [512, 256], replicated, may hold values from -0.375 to 0.375
- b_in: float32 [512], replicated, may hold values from -3 to 3
- w_out: bfloat16 [256, 512], replicated, may hold values from -0.25 to 0.25
- kernel: float32 [256, 9], P('chan'), may hold values from -4 to 4
Outputs:
- spec_out: bfloat16 [384, 1, 256, 2, 384], P('lat', None, 'chan')
Inputs may be any that keep to these rules, and one draw needn't show every extreme that they name: mode_slot holds every number of 0 to 383 once.
All inputs are finite; a program needn't handle non-finite values.
Results may differ from a plain program's by a relative error of at most 0.0083.
Values may be sent and summed in bfloat16 or wider, within the bound.
A program may use at most 64 MiB of HBM per device.

v0:
```python
import math

import jax
import jax.numpy as jnp
from jax import lax
from jax.sharding import PartitionSpec as P

NLON = 768


def with_halo(array, sides, width):
    for axis, dim in sides:
        count, length = (lax.axis_size(axis), array.shape[dim])
        up = [(i, (i + 1) % count) for i in range(count - 1)]
        down = [(j, i) for i, j in up]
        last = lax.slice_in_dim(array, length - width, length, axis=dim)
        first = lax.slice_in_dim(array, 0, width, axis=dim)
        before = lax.ppermute(last, axis, up)
        after = lax.ppermute(first, axis, down)
        array = jnp.concatenate([before, array, after], axis=dim)
    return array


def wave_table(modes, count):
    columns = jnp.arange(count, dtype=jnp.int32)
    phase = modes[:, None] * columns[None, :] % count
    angle = phase.astype(jnp.float32) * (2.0 * math.pi / count)
    factor = count ** (-0.5)
    return jnp.stack([jnp.cos(angle) * factor, -jnp.sin(angle) * factor], axis=1)


def on_device(spec_in, legendre, mode_slot, w_in, b_in, w_out, kernel):
    high = lax.Precision.HIGHEST
    slots_here = legendre.shape[0]
    lat_index = lax.axis_index("lat")
    local_modes = lax.dynamic_slice_in_dim(mode_slot, lat_index * slots_here, slots_here)
    degrees = jnp.arange(legendre.shape[2], dtype=jnp.int32)
    masked = jnp.where(
        degrees[None, None, :] >= local_modes[:, None, None], legendre, jnp.float32(0.0)
    )
    waves = wave_table(mode_slot, NLON)
    coeff = jnp.einsum("sbcrl,stl->sbcrt", spec_in.astype(jnp.float32), masked, precision=high)
    grid = jnp.einsum(
        "sbcrt,srp->btcp",
        lax.all_to_all(
            coeff.astype(jnp.bfloat16), "lat", split_axis=4, concat_axis=0, tiled=True
        ).astype(coeff.dtype),
        waves,
        precision=high,
    ).astype(jnp.bfloat16)
    batch, rows_here, chan_here, columns = grid.shape
    points = lax.all_to_all(grid, "chan", split_axis=3, concat_axis=2, tiled=True)
    pre = jnp.einsum("hc,btcp->bthp", w_in, points, preferred_element_type=jnp.float32)
    hidden = jax.nn.gelu(pre + b_in[None, None, :, None], approximate=True).astype(jnp.bfloat16)
    branch = jnp.einsum("ch,bthp->btcp", w_out, hidden, preferred_element_type=jnp.float32)
    updated = (points.astype(jnp.float32) + branch).astype(jnp.bfloat16)
    mixed = lax.all_to_all(updated, "chan", split_axis=2, concat_axis=3, tiled=True)
    half = columns // 2
    last_row = lax.axis_size("lat") - 1
    padded = with_halo(mixed, (("lat", 1),), 1)
    upper = jnp.where(lat_index == 0, jnp.roll(mixed[:, 0:1], half, axis=3), padded[:, 0:1])
    lower = jnp.where(lat_index == last_row, jnp.roll(mixed[:, -1:], half, axis=3), padded[:, -1:])
    stacked = jnp.concatenate([upper, padded[:, 1:-1], lower], axis=1).astype(jnp.float32)
    wide = mixed.astype(jnp.float32)
    conv = jnp.zeros_like(wide)
    for i in range(3):
        band = stacked[:, i : i + rows_here]
        for j in range(3):
            conv = conv + kernel[:, 3 * i + j][None, None, :, None] * jnp.roll(band, 1 - j, axis=3)
    field = wide + conv
    modes = jnp.einsum("btcp,srp->sbcrt", field, waves, precision=high)
    return jnp.einsum(
        "sbcrt,stl->sbcrl",
        lax.all_to_all(
            modes.astype(jnp.bfloat16), "lat", split_axis=0, concat_axis=4, tiled=True
        ).astype(modes.dtype),
        masked,
        precision=high,
    ).astype(jnp.bfloat16)


def solution(mesh):
    in_specs = (
        P("lat", None, "chan", None, None),
        P("lat", None, None),
        P(),
        P(),
        P(),
        P(),
        P("chan", None),
    )
    out_specs = P("lat", None, "chan", None, None)
    return jax.shard_map(
        on_device, mesh=mesh, in_specs=in_specs, out_specs=out_specs, check_vma=False
    )
```

profile of v0, /device:TPU:1, one launch (start us, length us, event | category | flops | bytes accessed | tf_op | source)
XLA Modules:
  0.0 132.0 jit_solution(14984198098485839276)
XLA Ops:
  0.0 0.8 dynamic_slice.3
  0.8 0.1 iota_compare_fusion
  0.9 0.1 copy-done
  1.0 4.2 %fusion.54 = bf16[6,1,32,2,384]{4,2,3,0,1:T(8,128)(2,1)S(1)} fusion(f32[6,384,384]{2,1,0:T(8,128)} %param.8, pred[6,384]{1,0:T(8,128)(4,1)S(1)} %iota_compare_fusion, bf16[6,32,2,384]{3,2,1,0:T(2,128)(2,1)S(1)} %bitcast.147), kind=kOutput, calls=%fused_computation.48 | convolution fusion | flops 680509440 | bytes 4131072 | tf_op jit(solution)/shard_map/sbcrl,stl->sbcrt/dot_general | solution.py:42
  5.2 1.2 copy.58
  6.5 0.0 copy-start.6
  6.5 1.9 %reshape.418 = bf16[64,2,1152]{2,1,0:T(2,128)(2,1)} reshape(bf16[384,1,6,2,32]{4,3,2,1,0:T(2,128)(2,1)S(1)} %bitcast.151) | data formatting | bytes 589824
  8.3 14.8 %all-to-all-start = ((bf16[64,2,1152]{2,1,0:T(2,128)(2,1)}), bf16[64,2,1152]{2,1,0:T(2,128)(2,1)S(1)}, u32[]{:S(2)}, u32[]{:S(2)}) async-start(bf16[64,2,1152]{2,1,0:T(2,128)(2,1)} %reshape.418), calls=%async_computation | async-start | bytes 589824 | tf_op jit(solution)/shard_map/all_to_all | solution.py:45
  23.2 6.1 %cosine_multiply_fusion = (f32[384,1,768]{2,0,1:T(8,128)S(1)}, f32[384,1,768]{2,0,1:T(8,128)}) fusion(s32[384]{0:T(512)S(1)} %copy-done.6), kind=kLoop, calls=%fused_computation.42 | loop fusion | flops 3538944 | bytes 2360832 | tf_op jit(solution)/shard_map/mul | solution.py:29
  29.3 6.5 %all-to-all-done = bf16[64,2,1152]{2,1,0:T(2,128)(2,1)S(1)} async-done(((bf16[64,2,1152]{2,1,0:T(2,128)(2,1)}), bf16[64,2,1152]{2,1,0:T(2,128)(2,1)S(1)}, u32[]{:S(2)}, u32[]{:S(2)}) %all-to-all-start) | async-done | bytes 294944 | tf_op jit(solution)/shard_map/all_to_all | solution.py:45
  35.8 0.7 reshape.419
  36.5 0.8 copy.59
  37.3 0.8 copy.60
  38.1 0.4 copy-done.3
  38.6 1.6 %fusion.60 = bf16[1,6,32,768]{3,2,1,0:T(8,128)(2,1)S(1)} fusion(bf16[384,32,2,6]{1,2,3,0:T(2,128)(2,1)S(1)} %bitcast.158, f32[384,1,768]{2,0,1:T(8,128)S(1)} %copy-done.3, f32[384,1,768]{2,0,1:T(8,128)S(1)} %get-tuple-element.32), kind=kOutput, calls=%fused_computation.50 | convolution fusion | flops 1359691776 | bytes 2949120 | tf_op jit(solution)/shard_map/sbcrt,srp->btcp/dot_general | solution.py:43
  40.1 1.1 copy.62
  41.2 1.2 reshape.420
  42.4 18.8 %all_to_all.63 = bf16[8,2,9216]{2,1,0:T(2,128)(2,1)S(1)} all-to-all(bf16[8,2,9216]{2,1,0:T(2,128)(2,1)S(1)} %reshape.420), channel_id=1, replica_groups=mesh['lat'=64,'chan'=8] {'chan'}, dimensions={0} | all-to-all | bytes 589824 | tf_op jit(solution)/shard_map/all_to_all | solution.py:52
  61.2 1.0 reshape.421
  62.2 1.0 copy.63
  63.2 0.0 copy-start.7
  63.3 0.1 bitcast_convert_fusion
  63.3 0.3 copy.65
  63.6 0.6 copy-done.7
  64.2 0.1 copy-done.8
  64.3 0.7 fusion.20
  65.0 1.1 copy.66
  66.1 3.5 %all-to-all-start.2 = ((bf16[1,6,256,96]{3,1,0,2:T(8,128)(2,1)}), bf16[1,6,256,96]{3,1,0,2:T(8,128)(2,1)S(1)}, u32[]{:S(2)}, u32[]{:S(2)}) async-start(bf16[1,6,256,96]{3,1,0,2:T(8,128)(2,1)} %copy.66), calls=%async_computation.2 | async-start | bytes 1048576 | tf_op jit(solution)/shard_map/all_to_all | solution.py:57
  69.6 16.6 %all-to-all-done.2 = bf16[1,6,256,96]{3,1,0,2:T(8,128)(2,1)S(1)} async-done(((bf16[1,6,256,96]{3,1,0,2:T(8,128)(2,1)}), bf16[1,6,256,96]{3,1,0,2:T(8,128)(2,1)S(1)}, u32[]{:S(2)}, u32[]{:S(2)}) %all-to-all-start.2) | async-done | bytes 294944 | tf_op jit(solution)/shard_map/all_to_all | solution.py:57
  86.3 0.1 copy.67
  86.3 0.2 copy.68
  86.5 0.3 all_to_all.55
  86.8 4.4 %collective-permute-start = (bf16[1,1,32,768]{3,2,1,0:T(8,128)(2,1)S(1)}, bf16[1,1,32,768]{3,2,1,0:T(8,128)(2,1)S(1)}, u32[]{:S(2)}, u32[]{:S(2)}) collective-permute-start(bf16[1,1,32,768]{3,2,1,0:T(8,128)(2,1)S(1)} %get-tuple-element.21), channel_id=1, source_target_pairs={{0,8},{8,16},{16,24},{24,32},{32,40},{40,48},{48,56},{56,64},{64,7... | collective-permute-start | bytes 147464 | tf_op jit(solution)/shard_map/ppermute | solution.py:18
  91.3 1.9 %collective-permute-start.1 = (bf16[1,1,32,768]{3,2,1,0:T(8,128)(2,1)S(1)}, bf16[1,1,32,768]{3,2,1,0:T(8,128)(2,1)S(1)}, u32[]{:S(2)}, u32[]{:S(2)}) collective-permute-start(bf16[1,1,32,768]{3,2,1,0:T(8,128)(2,1)S(1)} %get-tuple-element.22), channel_id=1, source_target_pairs={{8,0},{16,8},{24,16},{32,24},{40,32},{48,40},{56,48},{64,56},{72,6... | collective-permute-start | bytes 147464 | tf_op jit(solution)/shard_map/ppermute | solution.py:19
  93.2 3.4 %collective-permute-done.1 = bf16[1,1,32,768]{3,2,1,0:T(8,128)(2,1)S(1)} collective-permute-done((bf16[1,1,32,768]{3,2,1,0:T(8,128)(2,1)S(1)}, bf16[1,1,32,768]{3,2,1,0:T(8,128)(2,1)S(1)}, u32[]{:S(2)}, u32[]{:S(2)}) %collective-permute-start.1) | collective-permute-done | bytes 49184 | tf_op jit(solution)/shard_map/ppermute | solution.py:19
  96.7 0.1 maximum_convert_fusion
  96.8 0.1 fusion.118
  96.9 0.6 fusion.117
  97.6 0.6 copy-done.2
  98.2 0.4 copy-done.4
  98.5 3.2 %fusion.57 = bf16[384,1,32,2,6]{0,2,4,3,1:T(8,128)(2,1)S(1)} fusion(f32[384,1,768]{2,0,1:T(8,128)S(1)} %copy-done.4, f32[384,1,768]{2,0,1:T(8,128)S(1)} %copy-done.2, f32[1,8,32,768]{3,2,1,0:T(8,128)S(1)} %maximum_convert_fusion, f32[1,6,32,767]{3,2,1,0:T(8,128)S(1)} %get-tuple-element.10, f32[1,6,32,1]{3,2,1,0:T(8,128)S(1)} %get-tuple-element.16, ...), kind=kOutput, calls=%fused_computation.49 | convolution fusion | flops 1363378176 | bytes 8851968 | tf_op jit(solution)/shard_map/btcp,srp->sbcrt/dot_general | solution.py:71
  101.8 1.3 copy.69
  103.1 1.1 reshape.422
  104.2 21.6 %all_to_all.64 = bf16[64,2,1152]{2,1,0:T(2,128)(2,1)S(1)} all-to-all(bf16[64,2,1152]{2,1,0:T(2,128)(2,1)S(1)} %reshape.422), channel_id=1, replica_groups=mesh['lat'=64,'chan'=8] {'lat'}, dimensions={0} | all-to-all | bytes 589824 | tf_op jit(solution)/shard_map/all_to_all | solution.py:74
  125.8 0.7 reshape.423
  126.5 0.8 copy.70
  127.3 3.7 %fusion.49 = bf16[6,1,32,2,384]{4,2,3,0,1:T(8,128)(2,1)S(1)} fusion(f32[6,384,384]{2,1,0:T(8,128)} %param.8, pred[6,384]{1,0:T(8,128)(4,1)S(1)} %iota_compare_fusion, bf16[6,32,2,384]{1,2,3,0:T(2,128)(2,1)S(1)} %bitcast.150), kind=kOutput, calls=%fused_computation.47 | convolution fusion | flops 680509440 | bytes 4131072 | tf_op jit(solution)/shard_map/sbcrt,stl->sbcrl/dot_general | solution.py:72
  131.0 0.9 copy.72
  (18 shorter events, 0.1 us)
Async XLA Ops:
  0.0 1.0 copy-start
  6.5 16.7 %copy-start.6 = (s32[384]{0:T(512)S(1)}, s32[384]{0:T(512)}, u32[]{:S(2)}) copy-start(s32[384]{0:T(512)} %param.9) | copy-start | bytes 4612
  8.3 27.5 %all-to-all-start = ((bf16[64,2,1152]{2,1,0:T(2,128)(2,1)}), bf16[64,2,1152]{2,1,0:T(2,128)(2,1)S(1)}, u32[]{:S(2)}, u32[]{:S(2)}) async-start(bf16[64,2,1152]{2,1,0:T(2,128)(2,1)} %reshape.418), calls=%async_computation | async-start | bytes 589824 | tf_op jit(solution)/shard_map/all_to_all | solution.py:45
  29.3 8.9 %copy-start.1 = (f32[384,1,768]{2,0,1:T(8,128)}, f32[384,1,768]{2,0,1:T(8,128)S(1)}, u32[]{:S(2)}) copy-start(f32[384,1,768]{2,0,1:T(8,128)S(1)} %get-tuple-element.32) | copy-start | bytes 3538948
  37.3 1.3 copy-start.3
  63.2 1.0 copy-start.7
  63.2 1.0 copy-start.8
  63.2 1.0 copy-start.9
  65.0 4.6 %copy-start.5 = (f32[32,9]{0,1:T(8,128)S(1)}, f32[32,9]{0,1:T(8,128)}, u32[]{:S(2)}) copy-start(f32[32,9]{0,1:T(8,128)} %param.13) | copy-start | bytes 3460
  66.1 20.2 %all-to-all-start.2 = ((bf16[1,6,256,96]{3,1,0,2:T(8,128)(2,1)}), bf16[1,6,256,96]{3,1,0,2:T(8,128)(2,1)S(1)}, u32[]{:S(2)}, u32[]{:S(2)}) async-start(bf16[1,6,256,96]{3,1,0,2:T(8,128)(2,1)} %copy.66), calls=%async_computation.2 | async-start | bytes 1048576 | tf_op jit(solution)/shard_map/all_to_all | solution.py:57
  86.8 6.4 %collective-permute-start = (bf16[1,1,32,768]{3,2,1,0:T(8,128)(2,1)S(1)}, bf16[1,1,32,768]{3,2,1,0:T(8,128)(2,1)S(1)}, u32[]{:S(2)}, u32[]{:S(2)}) collective-permute-start(bf16[1,1,32,768]{3,2,1,0:T(8,128)(2,1)S(1)} %get-tuple-element.21), channel_id=1, source_target_pairs={{0,8},{8,16},{16,24},{24,32},{32,40},{40,48},{48,56},{56,64},{64,7... | collective-permute-start | bytes 147464 | tf_op jit(solution)/shard_map/ppermute | solution.py:18
  91.3 5.4 %collective-permute-start.1 = (bf16[1,1,32,768]{3,2,1,0:T(8,128)(2,1)S(1)}, bf16[1,1,32,768]{3,2,1,0:T(8,128)(2,1)S(1)}, u32[]{:S(2)}, u32[]{:S(2)}) collective-permute-start(bf16[1,1,32,768]{3,2,1,0:T(8,128)(2,1)S(1)} %get-tuple-element.22), channel_id=1, source_target_pairs={{8,0},{16,8},{24,16},{32,24},{40,32},{48,40},{56,48},{64,56},{72,6... | collective-permute-start | bytes 147464 | tf_op jit(solution)/shard_map/ppermute | solution.py:19
  96.9 1.3 copy-start.2
  96.9 1.6 %copy-start.4 = (f32[384,1,768]{2,0,1:T(8,128)S(1)}, f32[384,1,768]{2,0,1:T(8,128)}, u32[]{:S(2)}) copy-start(f32[384,1,768]{2,0,1:T(8,128)} %get-tuple-element.33) | copy-start | bytes 3538948
where the time goes:
time: 132 us
  blocking collectives  40.4 us (31%)
  waiting for transfers between devices  26.6 us (20%)
  starting transfers between devices  24.6 us (19%)
  local copies, waits for them, and re-layouts  20.2 us (15%)
  matrix products  13.5 us (10%)
  other arithmetic  6.35 us (5%)
    all_to_all x1, blocking collectives, on_device(): lax.all_to_all(modes.astype(jnp.bfloat16), 'lat', split_axis=0, concat_ax...  21.6 us
    all_to_all x1, blocking collectives, on_device(): lax.all_to_all(grid, 'chan', split_axis=3, concat_axis=2, tiled=True)  18.8 us
    all_to_all x1, waiting for transfers between devices, on_device(): lax.all_to_all(updated, 'chan', split_axis=2, concat_axis=3, tiled=True)  16.6 us
    all_to_all x1, starting transfers between devices, on_device(): lax.all_to_all(coeff.astype(jnp.bfloat16), 'lat', split_axis=4, concat_ax...  14.8 us
    unnamed x26, local copies, waits for them, and re-layouts  8.78 us
    all_to_all x1, waiting for transfers between devices, on_device(): lax.all_to_all(coeff.astype(jnp.bfloat16), 'lat', split_axis=4, concat_ax...  6.52 us
    mul x1, other arithmetic, wave_table(): jnp.cos(angle) * factor  6.1 us
    ppermute x1, starting transfers between devices, with_halo(): before = lax.ppermute(last, axis, up)  4.41 us
  transfers between devices with their start and end apart: 4, of which 3 were waited for; matrix products, arithmetic and copies ran while one was open for 5% of the time, Pallas kernels for 0%

commit v1 on v0

v1 whole, which is shorter than its diff:
```python
import functools
import math

import jax
import jax.numpy as jnp
import numpy as np
from jax import lax
from jax.experimental import pallas as pl
from jax.experimental.pallas import tpu as pltpu
from jax.sharding import PartitionSpec as P

NLON = 768
MESH = pl.DeviceIdType.MESH
F32 = jnp.float32
BF16 = jnp.bfloat16
CHUNKS = (4, 2)
GRID3 = (4, 8, 2)
NT = (((1,), (1,)), ((), ()))
TN = (((0,), (0,)), ((), ()))
NN = (((1,), (0,)), ((), ()))


def dot(a, b, dims=NN, precision=None):
    return lax.dot_general(a, b, dims, preferred_element_type=F32, precision=precision)


def far_first(k, size):
    if size == 1:
        return 0 * k
    return size // 2 + (1 - 2 * (k % 2)) * ((k + 1) // 2)


def wave_constant(modes, count):
    phase = (np.arange(modes)[:, None] * np.arange(count)[None, :]) % count
    angle = phase * (2.0 * math.pi / count)
    factor = count ** -0.5
    return np.stack([np.cos(angle) * factor, -np.sin(angle) * factor]).astype(np.float32)


def iota(shape, dim):
    return lax.broadcasted_iota(jnp.int32, shape, dim)


def body(cfg, x_ref, leg_ref, table_ref, mode_ref, mode_row, w_in, b_in, w_out, kern, out_ref,
         legv, lb, tab, wvf, wv, *rest):
    lat_n, chan_n, grid3 = cfg
    chunks = CHUNKS
    nq = len(chunks)
    slots, _, cl, _, deg = x_ref.shape
    rows = sum(chunks)
    lanes_n = slots * 2 * cl
    ltiles = lanes_n // 128
    dtiles = deg // 128
    ptiles = NLON // 128
    cr = 2 * cl
    chans = cl * chan_n
    rest = list(rest)
    take = lambda n: [rest.pop(0) for _ in range(n)]
    scr, s1, r1, lt, g, r2, mx, r3, s4, r4 = (take(nq) for _ in range(10))
    leg_sem, tab_sem, sends, recvs, locs = rest

    lat = lax.axis_index("lat")
    chan = lax.axis_index("chan")

    leg_copies = [
        [pltpu.make_async_copy(leg_ref.at[s, :, pl.ds(128 * k, 128)], legv.at[s, k], leg_sem.at[s * dtiles + k]) for k in range(dtiles)]
        for s in range(slots)
    ]
    for per in leg_copies:
        for copy in per:
            copy.start()
    tab_copy = pltpu.make_async_copy(table_ref, tab, tab_sem)
    tab_copy.start()

    barrier = pltpu.get_barrier_semaphore()

    def lat_peer(k):
        nx, nz, nc = grid3
        kz, rem = k // (nx * nc), k % (nx * nc)
        kx, kc = rem // nc, rem % nc
        dz, dx, dc = far_first(kz, nz), far_first(kx, nx), (nc - 1) - kc
        x = (lat // (nz * nc) + dx) % nx
        z = ((lat // nc) % nz + dz) % nz
        c = (lat % nc + dc) % nc
        return (x * nz + z) * nc + c

    def chan_peer(k):
        return (chan + far_first(k, chan_n)) % chan_n

    def greet_lat(k, carry):
        pl.semaphore_signal(barrier, inc=1, device_id={"lat": lat_peer(k)}, device_id_type=MESH)
        return carry

    def greet_chan(k, carry):
        pl.semaphore_signal(barrier, inc=1, device_id={"chan": chan_peer(k)}, device_id_type=MESH)
        return carry

    lax.fori_loop(0, lat_n - 1, greet_lat, 0)
    lax.fori_loop(0, chan_n - 1, greet_chan, 0)

    def start_lat(q, src, dst, at):
        def one(k, carry):
            peer = lat_peer(k)
            pltpu.make_async_remote_copy(
                src_ref=src.at[peer], dst_ref=dst.at[lat], send_sem=sends.at[at], recv_sem=recvs.at[at],
                device_id={"lat": peer}, device_id_type=MESH,
            ).start()
            return carry

        lax.fori_loop(0, lat_n - 1, one, 0)
        pltpu.make_async_copy(src.at[lat], dst.at[lat], locs.at[at]).start()

    def wait_lat(q, src, dst, at):
        pltpu.make_async_copy(src.at[lat], dst.at[lat], locs.at[at]).wait()
        pltpu.make_async_remote_copy(
            src_ref=src.at[pl.ds(0, lat_n - 1)], dst_ref=dst.at[pl.ds(0, lat_n - 1)],
            send_sem=sends.at[at], recv_sem=recvs.at[at], device_id={"lat": (lat + 1) % lat_n}, device_id_type=MESH,
        ).wait()

    lane = iota((lat_n, 128), 1)
    col_x = iota((cr, cr), 1)
    row_x = iota((cr, cr), 0)
    split = (col_x == (row_x % cl) * 2 + row_x // cl).astype(BF16)
    merge = (col_x == (row_x % 2) * cl + row_x // 2).astype(BF16)
    pair = 128 // cr
    for first in range(0, slots, pair):
        parts = []
        for s in range(first, first + pair):
            m = mode_ref[lat * slots + s]
            for copy in leg_copies[s]:
                copy.wait()
            for j in range(rows):
                for k in range(dtiles):
                    piece = legv[s, k, pl.ds(j, lat_n, stride=rows), :]
                    piece = jnp.where(lane + 128 * k >= m, piece, 0.0)
                    lb[s, j * lat_n : (j + 1) * lat_n, 128 * k : 128 * (k + 1)] = piece.astype(BF16)
            xs = dot(split, x_ref[s, 0].reshape(cr, deg)).astype(BF16)
            parts.append(dot(lb[s], xs, NT))
        both = jnp.concatenate(parts, axis=1)
        j = 0
        for q, nj in enumerate(chunks):
            for jj in range(nj):
                scr[q][first // pair, pl.ds(jj, lat_n, stride=nj), :] = both[j * lat_n : (j + 1) * lat_n]
                j += 1

    def message(q):
        nj = chunks[q]
        value = jnp.concatenate([scr[q][k] for k in range(ltiles)], axis=1)
        return value.reshape(lat_n, nj, lanes_n).astype(BF16)

    def unpack(q, received):
        nj = chunks[q]
        value = received[...].astype(F32).reshape(lat_n * nj, lanes_n)
        for k in range(ltiles):
            scr[q][k] = value[:, 128 * k : 128 * (k + 1)]
        return [
            jnp.concatenate([scr[q][k, pl.ds(jj, lat_n, stride=nj), :] for k in range(ltiles)], axis=1)
            for jj in range(nj)
        ]

    for q in range(nq):
        s1[q][...] = message(q)
    pl.semaphore_wait(barrier, lat_n - 1 + chan_n - 1)
    for q in range(nq):
        start_lat(q, s1[q], r1[q], q)

    tab_copy.wait()
    n_modes = mode_row.shape[1]
    pick = (iota((n_modes, n_modes), 0) == mode_row[...]).astype(BF16)
    for r in range(2):
        chosen = dot(pick, tab[r], TN)
        for k in range(ptiles):
            wvf[k] = chosen[:, 128 * k : 128 * (k + 1)]
        for s in range(slots):
            for k in range(ptiles):
                wv[(s * 2 + r) * lat_n : (s * 2 + r + 1) * lat_n, 128 * k : 128 * (k + 1)] = wvf[
                    k, pl.ds(s, lat_n, stride=slots), :
                ].astype(BF16)

    lane_all = iota((1, lanes_n), 1)
    mode_lane = jnp.zeros((1, lanes_n), jnp.int32)
    for s in range(slots):
        mode_lane = jnp.where(lane_all // cr == s, mode_ref[lat * slots + s], mode_lane)
    theta = mode_lane.astype(F32) * (2.0 * math.pi / NLON)
    cos_m, sin_m = jnp.cos(theta), jnp.sin(theta)
    half_turn = jnp.where(mode_lane % 2 == 0, 1.0, -1.0).astype(F32)
    spread = (iota((cl, lanes_n), 1) % cl == iota((cl, lanes_n), 0)).astype(F32)
    taps = dot(kern[...], spread, TN, precision=lax.Precision.HIGHEST)
    part_sign = jnp.where((lane_all // cl) % 2 == 0, -1.0, 1.0).astype(F32)
    direct, crossed = [], []
    for i in range(3):
        left, mid, right = (taps[3 * i + n : 3 * i + n + 1] for n in range(3))
        direct.append((left + right) * cos_m + mid + (1.0 if i == 1 else 0.0))
        crossed.append((right - left) * sin_m * part_sign)

    bias = jnp.broadcast_to(b_in[...], (128, b_in.shape[1])).T

    def slots_of(q):
        return -(-chunks[q] * ptiles // chan_n)

    def exact_chan(q):
        return chunks[q] * ptiles - (slots_of(q) - 1) * chan_n

    def chan_copies(q, src_of, dst_of, at, full_of):
        n = slots_of(q)
        even = exact_chan(q) == chan_n

        def run(act):
            for k in range(chan_n - 1):
                peer = chan_peer(k)
                count = lambda size: act(
                    pltpu.make_async_remote_copy(
                        src_ref=src_of(peer, size), dst_ref=dst_of(size), send_sem=sends.at[at],
                        recv_sem=recvs.at[at], device_id={"chan": peer}, device_id_type=MESH,
                    )
                )
                if even:
                    count(n)
                else:
                    full = full_of(peer)

                    @pl.when(full)
                    def _():
                        count(n)

                    @pl.when(jnp.logical_not(full))
                    def _():
                        count(n - 1)

        return run

    def grid_src(q):
        return lambda peer, size: g[q].at[pl.ds(peer * slots_of(q), size)]

    def start_points(q):
        at = nq + q
        extra = exact_chan(q)
        chan_copies(
            q, grid_src(q),
            lambda size: r2[q].at[pl.ds(0, size), pl.ds(pl.multiple_of(chan * cl, cl), cl)],
            at, lambda peer: peer < extra,
        )(lambda copy: copy.start())
        n = slots_of(q)

        def own(size):
            pltpu.make_async_copy(
                g[q].at[pl.ds(chan * slots_of(q), size)],
                r2[q].at[pl.ds(0, size), pl.ds(pl.multiple_of(chan * cl, cl), cl)], locs.at[at],
            ).start()

        by_size(q, own)

    def by_size(q, act):
        n, extra = slots_of(q), exact_chan(q)
        if extra == chan_n:
            act(n)
        else:

            @pl.when(chan < extra)
            def _():
                act(n)

            @pl.when(chan >= extra)
            def _():
                act(n - 1)

    def wait_points(q):
        at = nq + q

        def act(size):
            span = (chan_n - 1) * cl
            pltpu.make_async_copy(
                g[q].at[pl.ds(chan * slots_of(q), size)],
                r2[q].at[pl.ds(0, size), pl.ds(pl.multiple_of(chan * cl, cl), cl)], locs.at[at],
            ).wait()
            pltpu.make_async_remote_copy(
                src_ref=r2[q].at[pl.ds(0, size), pl.ds(0, span)], dst_ref=r2[q].at[pl.ds(0, size), pl.ds(0, span)],
                send_sem=sends.at[at], recv_sem=recvs.at[at], device_id={"chan": (chan + 1) % chan_n}, device_id_type=MESH,
            ).wait_recv()

        by_size(q, act)

    def drain_sent(q, at, buffer):
        total = chunks[q] * ptiles

        def act(size):
            part = buffer.at[pl.ds(0, total - size)]
            pltpu.make_async_remote_copy(
                src_ref=part, dst_ref=part, send_sem=sends.at[at], recv_sem=recvs.at[at],
                device_id={"chan": (chan + 1) % chan_n}, device_id_type=MESH,
            ).wait_send()

        by_size(q, act)

    def start_mixed(q):
        at = 2 * nq + q

        def act(size):
            for k in range(chan_n - 1):
                peer = chan_peer(k)
                pltpu.make_async_remote_copy(
                    src_ref=mx[q].at[pl.ds(peer * slots_of(q), size)], dst_ref=r3[q].at[pl.ds(chan * slots_of(q), size)],
                    send_sem=sends.at[at], recv_sem=recvs.at[at], device_id={"chan": peer}, device_id_type=MESH,
                ).start()
            pltpu.make_async_copy(
                mx[q].at[pl.ds(chan * slots_of(q), size)], r3[q].at[pl.ds(chan * slots_of(q), size)], locs.at[at]
            ).start()

        by_size(q, act)

    def wait_mixed(q):
        at = 2 * nq + q
        total = chunks[q] * ptiles

        def act(size):
            pltpu.make_async_copy(
                mx[q].at[pl.ds(chan * slots_of(q), size)], r3[q].at[pl.ds(chan * slots_of(q), size)], locs.at[at]
            ).wait()
            peer = {"chan": (chan + 1) % chan_n}
            sent = mx[q].at[pl.ds(0, (chan_n - 1) * size)]
            pltpu.make_async_remote_copy(
                src_ref=sent, dst_ref=sent, send_sem=sends.at[at], recv_sem=recvs.at[at], device_id=peer, device_id_type=MESH,
            ).wait_send()
            got = r3[q].at[pl.ds(0, total - size)]
            pltpu.make_async_remote_copy(
                src_ref=got, dst_ref=got, send_sem=sends.at[at], recv_sem=recvs.at[at], device_id=peer, device_id_type=MESH,
            ).wait_recv()

        by_size(q, act)

    for q, nj in enumerate(chunks):
        wait_lat(q, s1[q], r1[q], q)
        parts = unpack(q, r1[q])
        for sr in range(2 * slots):
            lt[q][sr * lat_n : (sr + 1) * lat_n, :] = jnp.concatenate(
                [part[:, cl * sr : cl * (sr + 1)] for part in parts], axis=1
            ).astype(BF16)
        grid = dot(lt[q][...], wv[...], TN).astype(BF16)
        for jj in range(nj):
            for k in range(ptiles):
                tile = jj * ptiles + k
                g[q][(tile % chan_n) * slots_of(q) + tile // chan_n] = grid[cl * jj : cl * (jj + 1), 128 * k : 128 * (k + 1)]
        start_points(q)

    for q, nj in enumerate(chunks):
        wait_points(q)
        for n in range(slots_of(q)):
            points = r2[q][n]
            pre = dot(w_in[...], points)
            hidden = jax.nn.gelu(pre + bias, approximate=True).astype(BF16)
            mixed = (points.astype(F32) + dot(w_out[...], hidden)).astype(BF16)
            for dest in range(chan_n):
                mx[q][dest * slots_of(q) + n] = mixed[cl * dest : cl * (dest + 1)]
        start_mixed(q)

    for q, nj in enumerate(chunks):
        wait_mixed(q)
        field = []
        for jj in range(nj):
            tiles = [jj * ptiles + k for k in range(ptiles)]
            field.append(jnp.concatenate([r3[q][(tile % chan_n) * slots_of(q) + tile // chan_n] for tile in tiles], axis=1))
        modes = dot(wv[...], jnp.concatenate(field, axis=0), NT)
        for jj in range(nj):
            value = jnp.concatenate(
                [modes[lat_n * sr : lat_n * (sr + 1), cl * jj : cl * (jj + 1)] for sr in range(2 * slots)], axis=1
            )
            for k in range(ltiles):
                scr[q][k, pl.ds(jj, lat_n, stride=nj), :] = value[:, 128 * k : 128 * (k + 1)]
        s4[q][...] = message(q)
        start_lat(q, s4[q], r4[q], 3 * nq + q)

    values = []
    for q in range(nq):
        wait_lat(q, s4[q], r4[q], 3 * nq + q)
        values += unpack(q, r4[q])
    row = iota((lat_n, lanes_n), 0)
    before_first = jnp.where(row == 0, half_turn * values[0], pltpu.roll(values[-1], 1, 0))
    after_last = jnp.where(row == lat_n - 1, half_turn * values[-1], pltpu.roll(values[0], lat_n - 1, 0))
    around = [before_first] + values + [after_last]
    low = (iota((lat_n, 128), 1) // cl) % 2 == 0

    def swap(a):
        pieces = []
        for k in range(ltiles):
            piece = a[:, 128 * k : 128 * (k + 1)]
            pieces.append(jnp.where(low, pltpu.roll(piece, 128 - cl, 1), pltpu.roll(piece, cl, 1)))
        return jnp.concatenate(pieces, axis=1)

    result = []
    for j in range(rows):
        straight = sum(direct[i] * around[j + i] for i in range(3))
        turned = sum(crossed[i] * swap(around[j + i]) for i in range(3))
        result.append((straight + turned).astype(BF16))
    stacked = jnp.concatenate(result, axis=0)
    for first in range(0, slots, pair):
        flipped = stacked[:, first * cr : (first + pair) * cr].T
        for s in range(first, first + pair):
            spec = dot(flipped[(s - first) * cr : (s - first + 1) * cr], lb[s]).astype(BF16)
            out_ref[s, 0] = dot(merge, spec).astype(BF16).reshape(cl, 2, deg)

    for q in range(nq):
        drain_sent(q, nq + q, g[q])


def block(cfg, table, spec_in, legendre, mode_slot, w_in, b_in, w_out, kernel):
    lat_n, chan_n, _ = cfg
    slots, batch, cl, _, deg = spec_in.shape
    rows = legendre.shape[1] // lat_n
    lanes_n = slots * 2 * cl
    n_modes = mode_slot.shape[0]
    ptiles = NLON // 128
    width = [-(-n * ptiles // chan_n) for n in CHUNKS]
    both = list(zip(CHUNKS, width))
    vm = pl.BlockSpec(memory_space=pltpu.VMEM)
    hbm = pl.BlockSpec(memory_space=pl.ANY)
    scratch = [
        pltpu.VMEM((slots, deg // 128, legendre.shape[1], 128), F32),
        pltpu.VMEM((slots, legendre.shape[1], deg), BF16),
        pltpu.VMEM((2, n_modes, NLON), BF16),
        pltpu.VMEM((ptiles, n_modes, 128), F32),
        pltpu.VMEM((2 * n_modes, NLON), BF16),
    ]
    message = lambda: [pltpu.VMEM((lat_n, n, lanes_n), BF16) for n in CHUNKS]
    scratch += [pltpu.VMEM((lanes_n // 128, lat_n * n, 128), F32) for n in CHUNKS]
    scratch += message() + message()
    scratch += [pltpu.VMEM((2 * n_modes, cl * n), BF16) for n in CHUNKS]
    scratch += [pltpu.VMEM((chan_n * t, cl, 128), BF16) for n, t in both]
    scratch += [pltpu.VMEM((t, chan_n * cl, 128), BF16) for n, t in both]
    scratch += [pltpu.VMEM((chan_n * t, cl, 128), BF16) for n, t in both]
    scratch += [pltpu.VMEM((chan_n * t, cl, 128), BF16) for n, t in both]
    scratch += message() + message()
    nq = len(CHUNKS)
    scratch += [
        pltpu.SemaphoreType.DMA((slots * deg // 128,)),
        pltpu.SemaphoreType.DMA,
        pltpu.SemaphoreType.DMA((4 * nq,)),
        pltpu.SemaphoreType.DMA((4 * nq,)),
        pltpu.SemaphoreType.DMA((4 * nq,)),
    ]
    return pl.pallas_call(
        functools.partial(body, cfg),
        out_shape=jax.ShapeDtypeStruct(spec_in.shape, BF16),
        in_specs=[vm, hbm, hbm, pl.BlockSpec(memory_space=pltpu.SMEM), vm, vm, vm, vm, vm],
        out_specs=vm,
        scratch_shapes=scratch,
        compiler_params=pltpu.CompilerParams(
            collective_id=0, has_side_effects=True, vmem_limit_bytes=60 * 1024 * 1024
        ),
        name="spherical_block",
    )(
        spec_in, legendre, jnp.asarray(table, BF16), mode_slot, mode_slot.reshape(1, -1), w_in,
        b_in.reshape(1, -1), w_out, kernel,
    )


def solution(mesh, grid3=GRID3, modes=384):
    in_specs = (
        P("lat", None, "chan", None, None),
        P("lat", None, None),
        P(),
        P(),
        P(),
        P(),
        P("chan", None),
    )
    out_specs = P("lat", None, "chan", None, None)
    cfg = (mesh.shape["lat"], mesh.shape["chan"], grid3)
    table = wave_constant(modes, NLON)
    return jax.shard_map(
        functools.partial(block, cfg, table), mesh=mesh, in_specs=in_specs, out_specs=out_specs, check_vma=False
    )
```

time: 132 us -> 62.2 us (0.47)
  Pallas kernels: 0 us -> 57.4 us
  blocking collectives: 40.4 us -> 0 us
  waiting for transfers between devices: 26.6 us -> 0 us
  starting transfers between devices: 24.6 us -> 0 us
  local copies, waits for them, and re-layouts: 20.2 us -> 4.53 us
  matrix products: 13.5 us -> 0 us
  other arithmetic: 6.35 us -> 0 us
    pallas_call x0 -> x1, Pallas kernels: none -> 57.4 us  [block(): pl.pallas_call(functools.partial(body, cfg), out_shape=jax.ShapeDtypeStru...]
    all_to_all x2 -> x0, blocking collectives: 40.4 us -> none  [the longest x1 21.6 us: on_device(): lax.all_to_all(modes.astype(jnp.bfloat16), 'lat', split_axis=0, concat_ax...]
    all_to_all x2 -> x0, waiting for transfers between devices: 23.2 us -> none  [the longest x1 16.6 us: on_device(): lax.all_to_all(updated, 'chan', split_axis=2, concat_axis=3, tiled=True)]
    all_to_all x2 -> x0, starting transfers between devices: 18.3 us -> none  [the longest x1 14.8 us: on_device(): lax.all_to_all(coeff.astype(jnp.bfloat16), 'lat', split_axis=4, concat_ax...]
    dot_general x5 -> x0, matrix products: 13.5 us -> none  [the longest x1 4.23 us: on_device(): jnp.einsum('sbcrl,stl->sbcrt', spec_in.astype(jnp.float32), masked, preci...]
    ppermute x2 -> x0, starting transfers between devices: 6.33 us -> none  [the longest x1 4.41 us: with_halo(): before = lax.ppermute(last, axis, up)]
    mul x1 -> x0, other arithmetic: 6.1 us -> none  [wave_table(): jnp.cos(angle) * factor]
    convert_element_type x6 -> x0, local copies, waits for them, and re-layouts: 5.87 us -> none  [the longest x2 1.35 us: on_device(): updated = (points.astype(jnp.float32) + branch).astype(jnp.bfloat16)]
  transfers between devices with their start and end apart: 4 -> 0, of which waited for: 3 -> 0; matrix products, arithmetic and copies ran while one was open for 5% -> 0% of each run, Pallas kernels for 0% -> 0%
where the time goes in v1:
time: 62.2 us; the launch traced here: 61.9 us
  Pallas kernels  57.4 us (92%)
  local copies, waits for them, and re-layouts  4.53 us (7%)
    pallas_call x1, Pallas kernels, block(): pl.pallas_call(functools.partial(body, cfg), out_shape=jax.ShapeDtypeStru...  57.4 us
    unnamed x2, local copies, waits for them, and re-layouts  3.26 us
    reshape x1, local copies, waits for them, and re-layouts, block(): mode_slot.reshape(1, -1)  1.28 us

profile of v1, /device:TPU:1, one launch (start us, length us, event | category | flops | bytes accessed | tf_op | source)
XLA Modules:
  0.0 61.9 jit_solution(13008638500211225675)
XLA Ops:
  0.0 1.3 %reshape.6.mode_row = s32[1,384]{1,0:T(1,128)} reshape(s32[384]{0:T(512)} %mode_ref.1) | data formatting | bytes 3072 | tf_op jit(solution)/shard_map/reshape | solution.py:451
  1.3 1.4 %copy.9.kern = f32[32,9]{1,0:T(8,128)} copy(f32[32,9]{0,1:T(8,128)} %param.14) | data formatting | bytes 2304 | tf_op args[6]
  2.7 57.4 %spherical_block.1 = bf16[6,1,32,2,384]{4,3,2,1,0:T(2,128)(2,1)} custom-call(bf16[6,1,32,2,384]{4,3,2,1,0:T(2,128)(2,1)} %x_ref.1, f32[6,384,384]{2,1,0:T(8,128)} %leg_ref.1, bf16[2,384,768]{2,1,0:T(8,128)(2,1)} %constant.2.clone.table_ref, s32[384]{0:T(512)} %mode_ref.1, s32[1,384]{1,0:T(1,128)} %reshape.6.mode_row, bf16[512,256]{1,0:T(8,128)(2,1)} %w_in.1, ...), custom_call_target="tpu_custom_call" | custom-call | tf_op jit(solution)/shard_map/spherical_block/pallas_call | solution.py:440
  60.0 1.9 %copy.11 = bf16[6,1,32,2,384]{4,3,2,1,0:T(2,128)(2,1)} copy(bf16[6,1,32,2,384]{4,3,2,1,0:T(2,128)(2,1)} %spherical_block.1) | data formatting | bytes 589824

commit v2 on v1

--- a/solution.py
+++ b/solution.py
@@ -13,7 +13,7 @@
 MESH = pl.DeviceIdType.MESH
 F32 = jnp.float32
 BF16 = jnp.bfloat16
-CHUNKS = (4, 2)
+CHUNKS = (2, 2, 2)
 GRID3 = (4, 8, 2)
 NT = (((1,), (1,)), ((), ()))
 TN = (((0,), (0,)), ((), ()))
@@ -41,8 +41,8 @@
     return lax.broadcasted_iota(jnp.int32, shape, dim)
 
 
-def body(cfg, x_ref, leg_ref, table_ref, mode_ref, mode_row, w_in, b_in, w_out, kern, out_ref,
-         legv, lb, tab, wvf, wv, *rest):
+def body(cfg, x_ref, leg_ref, table_ref, mode_hbm, w_in_ref, b_ref, w_out_ref, kern_ref, out_ref,
+         legv, lb, tab, wvf, wv, xv, mode_ref, mode_row, w_in, b_in, w_out, kern, *rest):
     lat_n, chan_n, grid3 = cfg
     chunks = CHUNKS
     nq = len(chunks)
@@ -57,57 +57,66 @@
     rest = list(rest)
     take = lambda n: [rest.pop(0) for _ in range(n)]
     scr, s1, r1, lt, g, r2, mx, r3, s4, r4 = (take(nq) for _ in range(10))
-    leg_sem, tab_sem, sends, recvs, locs = rest
+    leg_sem, in_sem, sends, recvs, locs = rest
 
     lat = lax.axis_index("lat")
     chan = lax.axis_index("chan")
 
-    leg_copies = [
-        [pltpu.make_async_copy(leg_ref.at[s, :, pl.ds(128 * k, 128)], legv.at[s, k], leg_sem.at[s * dtiles + k]) for k in range(dtiles)]
-        for s in range(slots)
+    first_row = [lat_n * sum(chunks[:q]) for q in range(nq)]
+    leg_copies = []
+    for q, nj in enumerate(chunks):
+        rows_q = pl.ds(first_row[q], lat_n * nj)
+        leg_copies.append(
+            [pltpu.make_async_copy(leg_ref.at[s, rows_q], legv.at[s, rows_q], leg_sem.at[q * slots + s]) for s in range(slots)]
+        )
+    in_copies = [
+        pltpu.make_async_copy(src, dst, in_sem.at[k])
+        for k, (src, dst) in enumerate(
+            [(x_ref, xv), (mode_hbm, mode_ref), (table_ref, tab), (mode_hbm, mode_row), (w_in_ref, w_in), (b_ref, b_in), (w_out_ref, w_out), (kern_ref, kern)]
+        )
     ]
-    for per in leg_copies:
+    barrier = pltpu.get_barrier_semaphore()
+
+    nx, nz, nc = grid3
+    here_x, here_z, here_c = lat // (nz * nc), (lat // nc) % nz, lat % nc
+    peer_x = [((here_x + far_first(k, nx)) % nx) * (nz * nc) for k in range(nx)]
+    peer_c = [(here_c + nc - 1 - k) % nc for k in range(nc)]
+    peer_xc = [x + c for x in peer_x for c in peer_c]
+    chan_peers = [(chan + far_first(k, chan_n)) % chan_n for k in range(chan_n - 1)]
+
+    def each_lat(act):
+        def at_z(k, carry):
+            z = ((here_z + far_first(k, nz)) % nz) * nc
+            for base in peer_xc:
+                act(base + z)
+            return carry
+
+        lax.fori_loop(0, nz - 1, at_z, 0)
+        for base in peer_xc[:-1]:
+            act(base + here_z * nc)
+
+    each_lat(lambda peer: pl.semaphore_signal(barrier, inc=1, device_id={"lat": peer}, device_id_type=MESH))
+    for peer in chan_peers:
+        pl.semaphore_signal(barrier, inc=1, device_id={"chan": peer}, device_id_type=MESH)
+    in_copies[0].start()
+    in_copies[1].start()
+    for copy in leg_copies[0]:
+        copy.start()
+    in_copies[2].start()
+    for per in leg_copies[1:]:
         for copy in per:
             copy.start()
-    tab_copy = pltpu.make_async_copy(table_ref, tab, tab_sem)
-    tab_copy.start()
-
-    barrier = pltpu.get_barrier_semaphore()
-
-    def lat_peer(k):
-        nx, nz, nc = grid3
-        kz, rem = k // (nx * nc), k % (nx * nc)
-        kx, kc = rem // nc, rem % nc
-        dz, dx, dc = far_first(kz, nz), far_first(kx, nx), (nc - 1) - kc
-        x = (lat // (nz * nc) + dx) % nx
-        z = ((lat // nc) % nz + dz) % nz
-        c = (lat % nc + dc) % nc
-        return (x * nz + z) * nc + c
-
-    def chan_peer(k):
-        return (chan + far_first(k, chan_n)) % chan_n
-
-    def greet_lat(k, carry):
-        pl.semaphore_signal(barrier, inc=1, device_id={"lat": lat_peer(k)}, device_id_type=MESH)
-        return carry
-
-    def greet_chan(k, carry):
-        pl.semaphore_signal(barrier, inc=1, device_id={"chan": chan_peer(k)}, device_id_type=MESH)
-        return carry
-
-    lax.fori_loop(0, lat_n - 1, greet_lat, 0)
-    lax.fori_loop(0, chan_n - 1, greet_chan, 0)
+    for copy in in_copies[3:]:
+        copy.start()
 
     def start_lat(q, src, dst, at):
-        def one(k, carry):
-            peer = lat_peer(k)
+        def one(peer):
             pltpu.make_async_remote_copy(
                 src_ref=src.at[peer], dst_ref=dst.at[lat], send_sem=sends.at[at], recv_sem=recvs.at[at],
                 device_id={"lat": peer}, device_id_type=MESH,
             ).start()
-            return carry
-
-        lax.fori_loop(0, lat_n - 1, one, 0)
+
+        each_lat(one)
         pltpu.make_async_copy(src.at[lat], dst.at[lat], locs.at[at]).start()
 
     def wait_lat(q, src, dst, at):
@@ -117,31 +126,11 @@
             send_sem=sends.at[at], recv_sem=recvs.at[at], device_id={"lat": (lat + 1) % lat_n}, device_id_type=MESH,
         ).wait()
 
-    lane = iota((lat_n, 128), 1)
     col_x = iota((cr, cr), 1)
     row_x = iota((cr, cr), 0)
     split = (col_x == (row_x % cl) * 2 + row_x // cl).astype(BF16)
     merge = (col_x == (row_x % 2) * cl + row_x // 2).astype(BF16)
     pair = 128 // cr
-    for first in range(0, slots, pair):
-        parts = []
-        for s in range(first, first + pair):
-            m = mode_ref[lat * slots + s]
-            for copy in leg_copies[s]:
-                copy.wait()
-            for j in range(rows):
-                for k in range(dtiles):
-                    piece = legv[s, k, pl.ds(j, lat_n, stride=rows), :]
-                    piece = jnp.where(lane + 128 * k >= m, piece, 0.0)
-                    lb[s, j * lat_n : (j + 1) * lat_n, 128 * k : 128 * (k + 1)] = piece.astype(BF16)
-            xs = dot(split, x_ref[s, 0].reshape(cr, deg)).astype(BF16)
-            parts.append(dot(lb[s], xs, NT))
-        both = jnp.concatenate(parts, axis=1)
-        j = 0
-        for q, nj in enumerate(chunks):
-            for jj in range(nj):
-                scr[q][first // pair, pl.ds(jj, lat_n, stride=nj), :] = both[j * lat_n : (j + 1) * lat_n]
-                j += 1
 
     def message(q):
         nj = chunks[q]
@@ -158,15 +147,31 @@
             for jj in range(nj)
         ]
 
-    for q in range(nq):
+    in_copies[0].wait()
+    in_copies[1].wait()
+    modes_here = [mode_ref[lat * slots + s] for s in range(slots)]
+    spectra = [dot(split, xv[s, 0].reshape(cr, deg)).astype(BF16) for s in range(slots)]
+    for q, nj in enumerate(chunks):
+        span = slice(first_row[q], first_row[q] + lat_n * nj)
+        degree = iota((lat_n * nj, deg), 1)
+        for first in range(0, slots, pair):
+            parts = []
+            for s in range(first, first + pair):
+                leg_copies[q][s].wait()
+                lb[s, span] = jnp.where(degree >= modes_here[s], legv[s, span], 0.0).astype(BF16)
+                parts.append(dot(lb[s, span], spectra[s], NT))
+            both = jnp.concatenate(parts, axis=1)
+            for jj in range(nj):
+                scr[q][first // pair, pl.ds(jj, lat_n, stride=nj), :] = both[jj * lat_n : (jj + 1) * lat_n]
         s1[q][...] = message(q)
-    pl.semaphore_wait(barrier, lat_n - 1 + chan_n - 1)
-    for q in range(nq):
+        if q == 0:
+            pl.semaphore_wait(barrier, lat_n - 1 + chan_n - 1)
         start_lat(q, s1[q], r1[q], q)
 
-    tab_copy.wait()
-    n_modes = mode_row.shape[1]
-    pick = (iota((n_modes, n_modes), 0) == mode_row[...]).astype(BF16)
+    for copy in in_copies[2:]:
+        copy.wait()
+    n_modes = mode_row.shape[0]
+    pick = (iota((n_modes, n_modes), 0) == mode_row[...].reshape(1, n_modes)).astype(BF16)
     for r in range(2):
         chosen = dot(pick, tab[r], TN)
         for k in range(ptiles):
@@ -185,7 +190,7 @@
     cos_m, sin_m = jnp.cos(theta), jnp.sin(theta)
     half_turn = jnp.where(mode_lane % 2 == 0, 1.0, -1.0).astype(F32)
     spread = (iota((cl, lanes_n), 1) % cl == iota((cl, lanes_n), 0)).astype(F32)
-    taps = dot(kern[...], spread, TN, precision=lax.Precision.HIGHEST)
+    taps = dot(kern[...], spread, precision=lax.Precision.HIGHEST)
     part_sign = jnp.where((lane_all // cl) % 2 == 0, -1.0, 1.0).astype(F32)
     direct, crossed = [], []
     for i in range(3):
@@ -201,13 +206,27 @@
     def exact_chan(q):
         return chunks[q] * ptiles - (slots_of(q) - 1) * chan_n
 
-    def chan_copies(q, src_of, dst_of, at, full_of):
+    def place(q, tile):
+        n, at = tile // chan_n, tile % chan_n
+        if n == slots_of(q) - 1 and 2 * exact_chan(q) == chan_n:
+            at = 2 * at + q % 2
+        return at, n
+
+    def is_full(q, who):
+        if 2 * exact_chan(q) == chan_n:
+            return who % 2 == q % 2
+        return who < exact_chan(q)
+
+    def flat(q, tile):
+        at, n = place(q, tile)
+        return at * slots_of(q) + n
+
+    def chan_copies(q, src_of, dst_of, at):
         n = slots_of(q)
         even = exact_chan(q) == chan_n
 
         def run(act):
-            for k in range(chan_n - 1):
-                peer = chan_peer(k)
+            for peer in chan_peers:
                 count = lambda size: act(
                     pltpu.make_async_remote_copy(
                         src_ref=src_of(peer, size), dst_ref=dst_of(size), send_sem=sends.at[at],
@@ -217,7 +236,7 @@
                 if even:
                     count(n)
                 else:
-                    full = full_of(peer)
+                    full = is_full(q, peer)
 
                     @pl.when(full)
                     def _():
@@ -234,11 +253,10 @@
 
     def start_points(q):
         at = nq + q
-        extra = exact_chan(q)
         chan_copies(
             q, grid_src(q),
             lambda size: r2[q].at[pl.ds(0, size), pl.ds(pl.multiple_of(chan * cl, cl), cl)],
-            at, lambda peer: peer < extra,
+            at,
         )(lambda copy: copy.start())
         n = slots_of(q)
 
@@ -251,16 +269,16 @@
         by_size(q, own)
 
     def by_size(q, act):
-        n, extra = slots_of(q), exact_chan(q)
-        if extra == chan_n:
+        n = slots_of(q)
+        if exact_chan(q) == chan_n:
             act(n)
         else:
 
-            @pl.when(chan < extra)
+            @pl.when(is_full(q, chan))
             def _():
                 act(n)
 
-            @pl.when(chan >= extra)
+            @pl.when(jnp.logical_not(is_full(q, chan)))
             def _():
                 act(n - 1)
 
@@ -296,8 +314,7 @@
         at = 2 * nq + q
 
         def act(size):
-            for k in range(chan_n - 1):
-                peer = chan_peer(k)
+            for peer in chan_peers:
                 pltpu.make_async_remote_copy(
                     src_ref=mx[q].at[pl.ds(peer * slots_of(q), size)], dst_ref=r3[q].at[pl.ds(chan * slots_of(q), size)],
                     send_sem=sends.at[at], recv_sem=recvs.at[at], device_id={"chan": peer}, device_id_type=MESH,
@@ -339,7 +356,7 @@
         for jj in range(nj):
             for k in range(ptiles):
                 tile = jj * ptiles + k
-                g[q][(tile % chan_n) * slots_of(q) + tile // chan_n] = grid[cl * jj : cl * (jj + 1), 128 * k : 128 * (k + 1)]
+                g[q][flat(q, tile)] = grid[cl * jj : cl * (jj + 1), 128 * k : 128 * (k + 1)]
         start_points(q)
 
     for q, nj in enumerate(chunks):
@@ -358,8 +375,8 @@
         field = []
         for jj in range(nj):
             tiles = [jj * ptiles + k for k in range(ptiles)]
-            field.append(jnp.concatenate([r3[q][(tile % chan_n) * slots_of(q) + tile // chan_n] for tile in tiles], axis=1))
-        modes = dot(wv[...], jnp.concatenate(field, axis=0), NT)
+            field.append(jnp.concatenate([r3[q][flat(q, tile)] for tile in tiles], axis=1))
+        modes = dot(jnp.concatenate(field, axis=0), wv[...], NT).T
         for jj in range(nj):
             value = jnp.concatenate(
                 [modes[lat_n * sr : lat_n * (sr + 1), cl * jj : cl * (jj + 1)] for sr in range(2 * slots)], axis=1
@@ -373,11 +390,12 @@
     for q in range(nq):
         wait_lat(q, s4[q], r4[q], 3 * nq + q)
         values += unpack(q, r4[q])
-    row = iota((lat_n, lanes_n), 0)
-    before_first = jnp.where(row == 0, half_turn * values[0], pltpu.roll(values[-1], 1, 0))
-    after_last = jnp.where(row == lat_n - 1, half_turn * values[-1], pltpu.roll(values[0], lat_n - 1, 0))
-    around = [before_first] + values + [after_last]
-    low = (iota((lat_n, 128), 1) // cl) % 2 == 0
+    n_rows = lat_n * rows
+    row = iota((n_rows, 1), 0)
+    here = jnp.concatenate(values, axis=0)
+    before = jnp.where(row == 0, half_turn * here, pltpu.roll(here, 1, 0))
+    after = jnp.where(row == n_rows - 1, half_turn * here, pltpu.roll(here, n_rows - 1, 0))
+    low = (iota((n_rows, 128), 1) // cl) % 2 == 0
 
     def swap(a):
         pieces = []
@@ -386,17 +404,14 @@
             pieces.append(jnp.where(low, pltpu.roll(piece, 128 - cl, 1), pltpu.roll(piece, cl, 1)))
         return jnp.concatenate(pieces, axis=1)
 
-    result = []
-    for j in range(rows):
-        straight = sum(direct[i] * around[j + i] for i in range(3))
-        turned = sum(crossed[i] * swap(around[j + i]) for i in range(3))
-        result.append((straight + turned).astype(BF16))
-    stacked = jnp.concatenate(result, axis=0)
+    straight = direct[0] * before + direct[1] * here + direct[2] * after
+    turned = crossed[0] * swap(before) + crossed[1] * swap(here) + crossed[2] * swap(after)
+    stacked = (straight + turned).astype(BF16)
     for first in range(0, slots, pair):
         flipped = stacked[:, first * cr : (first + pair) * cr].T
         for s in range(first, first + pair):
             spec = dot(flipped[(s - first) * cr : (s - first + 1) * cr], lb[s]).astype(BF16)
-            out_ref[s, 0] = dot(merge, spec).astype(BF16).reshape(cl, 2, deg)
+            out_ref[s] = dot(merge, spec).astype(BF16)
 
     for q in range(nq):
         drain_sent(q, nq + q, g[q])
@@ -412,13 +427,20 @@
     width = [-(-n * ptiles // chan_n) for n in CHUNKS]
     both = list(zip(CHUNKS, width))
     vm = pl.BlockSpec(memory_space=pltpu.VMEM)
-    hbm = pl.BlockSpec(memory_space=pl.ANY)
+    hbm = pl.BlockSpec(memory_space=pltpu.HBM)
     scratch = [
-        pltpu.VMEM((slots, deg // 128, legendre.shape[1], 128), F32),
+        pltpu.VMEM(legendre.shape, F32),
         pltpu.VMEM((slots, legendre.shape[1], deg), BF16),
         pltpu.VMEM((2, n_modes, NLON), BF16),
         pltpu.VMEM((ptiles, n_modes, 128), F32),
         pltpu.VMEM((2 * n_modes, NLON), BF16),
+        pltpu.VMEM(spec_in.shape, BF16),
+        pltpu.SMEM(mode_slot.shape, jnp.int32),
+        pltpu.VMEM(mode_slot.shape, jnp.int32),
+        pltpu.VMEM(w_in.shape, BF16),
+        pltpu.VMEM((1, b_in.shape[0]), F32),
+        pltpu.VMEM(w_out.shape, BF16),
+        pltpu.VMEM(kernel.shape[::-1], F32),
     ]
     message = lambda: [pltpu.VMEM((lat_n, n, lanes_n), BF16) for n in CHUNKS]
     scratch += [pltpu.VMEM((lanes_n // 128, lat_n * n, 128), F32) for n in CHUNKS]
@@ -431,16 +453,16 @@
     scratch += message() + message()
     nq = len(CHUNKS)
     scratch += [
-        pltpu.SemaphoreType.DMA((slots * deg // 128,)),
-        pltpu.SemaphoreType.DMA,
+        pltpu.SemaphoreType.DMA((slots * nq,)),
+        pltpu.SemaphoreType.DMA((8,)),
         pltpu.SemaphoreType.DMA((4 * nq,)),
         pltpu.SemaphoreType.DMA((4 * nq,)),
         pltpu.SemaphoreType.DMA((4 * nq,)),
     ]
     return pl.pallas_call(
         functools.partial(body, cfg),
-        out_shape=jax.ShapeDtypeStruct(spec_in.shape, BF16),
-        in_specs=[vm, hbm, hbm, pl.BlockSpec(memory_space=pltpu.SMEM), vm, vm, vm, vm, vm],
+        out_shape=jax.ShapeDtypeStruct((slots, 2 * cl, deg), BF16),
+        in_specs=[hbm] * 8,
         out_specs=vm,
         scratch_shapes=scratch,
         compiler_params=pltpu.CompilerParams(
@@ -448,9 +470,9 @@
         ),
         name="spherical_block",
     )(
-        spec_in, legendre, jnp.asarray(table, BF16), mode_slot, mode_slot.reshape(1, -1), w_in,
-        b_in.reshape(1, -1), w_out, kernel,
-    )
+        spec_in, legendre, jnp.asarray(table, BF16), mode_slot, w_in,
+        b_in.reshape(1, -1), w_out, kernel.T,
+    ).reshape(spec_in.shape)
 
 
 def solution(mesh, grid3=GRID3, modes=384):

time: 62.2 us -> 51.5 us (0.83)
  Pallas kernels: 57.4 us -> 49.5 us
  local copies, waits for them, and re-layouts: 4.53 us -> 1.79 us
    pallas_call x1, Pallas kernels: 57.4 us -> 49.5 us  [block(): pl.pallas_call(functools.partial(body, cfg), out_shape=jax.ShapeDtypeStru...]
    unnamed x2 -> x0, local copies, waits for them, and re-layouts: 3.26 us -> none
where the time goes in v2:
time: 51.5 us; the launch traced here: 51.3 us
  Pallas kernels  49.5 us (96%)
  local copies, waits for them, and re-layouts  1.79 us (3%)
    pallas_call x1, Pallas kernels, block(): pl.pallas_call(functools.partial(body, cfg), out_shape=jax.ShapeDtypeStru...  49.5 us
    reshape x1, local copies, waits for them, and re-layouts, block(): return pl.pallas_call(functools.partial(body, cfg), out_shape=jax.ShapeDt...  1.79 us

profile of v2, /device:TPU:1, one launch (start us, length us, event | category | flops | bytes accessed | tf_op | source)
XLA Modules:
  0.0 51.3 jit_solution(16180508724184874098)
XLA Ops:
  0.0 49.5 %spherical_block.1 = bf16[6,64,384]{2,1,0:T(8,128)(2,1)} custom-call(bf16[6,1,32,2,384]{4,3,2,1,0:T(2,128)(2,1)} %x_ref.1, f32[6,384,384]{2,1,0:T(8,128)} %leg_ref.1, bf16[2,384,768]{2,1,0:T(8,128)(2,1)} %constant.2.clone.table_ref, s32[384]{0:T(512)} %mode_hbm.1, bf16[512,256]{1,0:T(8,128)(2,1)} %w_in_ref.1, f32[1,512]{1,0:T(1,128)} %bitcast.4, ...), custom_call_target="tpu_custom_call" | custom-call | tf_op jit(solution)/shard_map/spherical_block/pallas_call | solution.py:462
  49.5 1.8 %reshape.7 = bf16[6,1,32,2,384]{4,3,2,0,1:T(2,128)(2,1)} reshape(bf16[6,64,384]{2,1,0:T(8,128)(2,1)} %spherical_block.1) | data formatting | bytes 589824 | tf_op jit(solution)/shard_map/reshape | solution.py:475

commit v3 on v2

--- a/solution.py
+++ b/solution.py
@@ -42,7 +42,7 @@
 
 
 def body(cfg, x_ref, leg_ref, table_ref, mode_hbm, w_in_ref, b_ref, w_out_ref, kern_ref, out_ref,
-         legv, lb, tab, wvf, wv, xv, mode_ref, mode_row, w_in, b_in, w_out, kern, *rest):
+         legv, lb, tab, wvf, wv, wvt, acc, xv, mode_ref, mode_row, w_in, b_in, w_out, kern, *rest):
     lat_n, chan_n, grid3 = cfg
     chunks = CHUNKS
     nq = len(chunks)
@@ -95,13 +95,14 @@
         for base in peer_xc[:-1]:
             act(base + here_z * nc)
 
-    each_lat(lambda peer: pl.semaphore_signal(barrier, inc=1, device_id={"lat": peer}, device_id_type=MESH))
-    for peer in chan_peers:
-        pl.semaphore_signal(barrier, inc=1, device_id={"chan": peer}, device_id_type=MESH)
     in_copies[0].start()
     in_copies[1].start()
     for copy in leg_copies[0]:
         copy.start()
+
+    each_lat(lambda peer: pl.semaphore_signal(barrier, inc=1, device_id={"lat": peer}, device_id_type=MESH))
+    for peer in chan_peers:
+        pl.semaphore_signal(barrier, inc=1, device_id={"chan": peer}, device_id_type=MESH)
     in_copies[2].start()
     for per in leg_copies[1:]:
         for copy in per:
@@ -129,8 +130,9 @@
     col_x = iota((cr, cr), 1)
     row_x = iota((cr, cr), 0)
     split = (col_x == (row_x % cl) * 2 + row_x // cl).astype(BF16)
-    merge = (col_x == (row_x % 2) * cl + row_x // 2).astype(BF16)
     pair = 128 // cr
+    wide_col, wide_row = iota((128, 128), 1), iota((128, 128), 0)
+    merge = (wide_col == wide_row // cr * cr + (wide_row % 2) * cl + wide_row % cr // 2).astype(BF16)
 
     def message(q):
         nj = chunks[q]
@@ -154,18 +156,19 @@
     for q, nj in enumerate(chunks):
         span = slice(first_row[q], first_row[q] + lat_n * nj)
         degree = iota((lat_n * nj, deg), 1)
+        for copy in leg_copies[q]:
+            copy.wait()
+        masked = [jnp.where(degree >= modes_here[s], legv[s, span], 0.0).astype(BF16) for s in range(slots)]
+        products = [dot(masked[s], spectra[s], NT) for s in range(slots)]
+        for s in range(slots):
+            lb[s, span] = masked[s]
         for first in range(0, slots, pair):
-            parts = []
-            for s in range(first, first + pair):
-                leg_copies[q][s].wait()
-                lb[s, span] = jnp.where(degree >= modes_here[s], legv[s, span], 0.0).astype(BF16)
-                parts.append(dot(lb[s, span], spectra[s], NT))
-            both = jnp.concatenate(parts, axis=1)
+            both = jnp.concatenate(products[first : first + pair], axis=1)
             for jj in range(nj):
                 scr[q][first // pair, pl.ds(jj, lat_n, stride=nj), :] = both[jj * lat_n : (jj + 1) * lat_n]
         s1[q][...] = message(q)
-        if q == 0:
-            pl.semaphore_wait(barrier, lat_n - 1 + chan_n - 1)
+    pl.semaphore_wait(barrier, lat_n - 1 + chan_n - 1)
+    for q in range(nq):
         start_lat(q, s1[q], r1[q], q)
 
     for copy in in_copies[2:]:
@@ -361,14 +364,18 @@
 
     for q, nj in enumerate(chunks):
         wait_points(q)
-        for n in range(slots_of(q)):
-            points = r2[q][n]
+        for n in range(0, slots_of(q), 2):
+            tiles = range(n, min(n + 2, slots_of(q)))
+            points = jnp.concatenate([r2[q][tile] for tile in tiles], axis=1)
             pre = dot(w_in[...], points)
-            hidden = jax.nn.gelu(pre + bias, approximate=True).astype(BF16)
+            hidden = jax.nn.gelu(pre + jnp.concatenate([bias for _ in tiles], axis=1), approximate=True).astype(BF16)
             mixed = (points.astype(F32) + dot(w_out[...], hidden)).astype(BF16)
             for dest in range(chan_n):
-                mx[q][dest * slots_of(q) + n] = mixed[cl * dest : cl * (dest + 1)]
+                for k, tile in enumerate(tiles):
+                    mx[q][dest * slots_of(q) + tile] = mixed[cl * dest : cl * (dest + 1), 128 * k : 128 * (k + 1)]
         start_mixed(q)
+
+    wvt[...] = wv[...].T
 
     for q, nj in enumerate(chunks):
         wait_mixed(q)
@@ -376,7 +383,7 @@
         for jj in range(nj):
             tiles = [jj * ptiles + k for k in range(ptiles)]
             field.append(jnp.concatenate([r3[q][flat(q, tile)] for tile in tiles], axis=1))
-        modes = dot(jnp.concatenate(field, axis=0), wv[...], NT).T
+        modes = dot(jnp.concatenate(field, axis=0), wvt[...]).T
         for jj in range(nj):
             value = jnp.concatenate(
                 [modes[lat_n * sr : lat_n * (sr + 1), cl * jj : cl * (jj + 1)] for sr in range(2 * slots)], axis=1
@@ -386,32 +393,45 @@
         s4[q][...] = message(q)
         start_lat(q, s4[q], r4[q], 3 * nq + q)
 
-    values = []
-    for q in range(nq):
-        wait_lat(q, s4[q], r4[q], 3 * nq + q)
-        values += unpack(q, r4[q])
-    n_rows = lat_n * rows
-    row = iota((n_rows, 1), 0)
-    here = jnp.concatenate(values, axis=0)
-    before = jnp.where(row == 0, half_turn * here, pltpu.roll(here, 1, 0))
-    after = jnp.where(row == n_rows - 1, half_turn * here, pltpu.roll(here, n_rows - 1, 0))
-    low = (iota((n_rows, 128), 1) // cl) % 2 == 0
-
     def swap(a):
+        low = (iota((a.shape[0], 128), 1) // cl) % 2 == 0
         pieces = []
         for k in range(ltiles):
             piece = a[:, 128 * k : 128 * (k + 1)]
             pieces.append(jnp.where(low, pltpu.roll(piece, 128 - cl, 1), pltpu.roll(piece, cl, 1)))
         return jnp.concatenate(pieces, axis=1)
 
-    straight = direct[0] * before + direct[1] * here + direct[2] * after
-    turned = crossed[0] * swap(before) + crossed[1] * swap(here) + crossed[2] * swap(after)
-    stacked = (straight + turned).astype(BF16)
-    for first in range(0, slots, pair):
-        flipped = stacked[:, first * cr : (first + pair) * cr].T
-        for s in range(first, first + pair):
-            spec = dot(flipped[(s - first) * cr : (s - first + 1) * cr], lb[s]).astype(BF16)
-            out_ref[s] = dot(merge, spec).astype(BF16)
+    edge = min(16, lat_n * chunks[0])
+    carried = None
+    for q, nj in enumerate(chunks):
+        wait_lat(q, s4[q], r4[q], 3 * nq + q)
+        here = jnp.concatenate(unpack(q, r4[q]), axis=0)
+        turned = swap(here)
+        to_next, own, to_last = (direct[i] * here + crossed[i] * turned for i in range(3))
+        n_rows = lat_n * nj
+        row = iota((n_rows, 1), 0)
+        from_last = half_turn * to_next[:1] if q == 0 else carried
+        from_next = half_turn * to_last[n_rows - 1 :] if q == nq - 1 else jnp.zeros_like(from_last)
+        carried = to_next[n_rows - 1 :]
+        field = own + jnp.where(row == 0, from_last, pltpu.roll(to_next, 1, 0))
+        field = field + jnp.where(row == n_rows - 1, from_next, pltpu.roll(to_last, n_rows - 1, 0))
+        field = field.astype(BF16)
+        start = first_row[q]
+        if q > 0:
+            missing = jnp.where(iota((edge, lanes_n), 0) == edge - 1, to_last[:1], 0.0).astype(BF16)
+            field = jnp.concatenate([missing, field], axis=0)
+            start -= edge
+        span = slice(start, first_row[q] + n_rows)
+        for first in range(0, slots, pair):
+            left = dot(merge, field[:, first * cr : (first + pair) * cr], NT).astype(BF16)
+            for s in range(first, first + pair):
+                part = dot(left[(s - first) * cr : (s - first + 1) * cr], lb[s, span])
+                if q > 0:
+                    part = part + acc[s]
+                if q < nq - 1:
+                    acc[s] = part
+                else:
+                    out_ref[s, 0] = part.astype(BF16).reshape(cl, 2, deg)
 
     for q in range(nq):
         drain_sent(q, nq + q, g[q])
@@ -434,6 +454,8 @@
         pltpu.VMEM((2, n_modes, NLON), BF16),
         pltpu.VMEM((ptiles, n_modes, 128), F32),
         pltpu.VMEM((2 * n_modes, NLON), BF16),
+        pltpu.VMEM((NLON, 2 * n_modes), BF16),
+        pltpu.VMEM((slots, 2 * cl, deg), F32),
         pltpu.VMEM(spec_in.shape, BF16),
         pltpu.SMEM(mode_slot.shape, jnp.int32),
         pltpu.VMEM(mode_slot.shape, jnp.int32),
@@ -461,7 +483,7 @@
     ]
     return pl.pallas_call(
         functools.partial(body, cfg),
-        out_shape=jax.ShapeDtypeStruct((slots, 2 * cl, deg), BF16),
+        out_shape=pltpu.VMEM(spec_in.shape, BF16),
         in_specs=[hbm] * 8,
         out_specs=vm,
         scratch_shapes=scratch,
@@ -472,7 +494,7 @@
     )(
         spec_in, legendre, jnp.asarray(table, BF16), mode_slot, w_in,
         b_in.reshape(1, -1), w_out, kernel.T,
-    ).reshape(spec_in.shape)
+    )
 
 
 def solution(mesh, grid3=GRID3, modes=384):

time: 51.5 us -> 48.6 us (0.944)
  Pallas kernels: 49.5 us -> 47.8 us
  local copies, waits for them, and re-layouts: 1.79 us -> 0.72 us
    reshape x1 -> x0, local copies, waits for them, and re-layouts: 1.79 us -> none  [block(): return pl.pallas_call(functools.partial(body, cfg), out_shape=jax.ShapeDt...]
    pallas_call x1, Pallas kernels: 49.5 us -> 47.8 us  [block(): pl.pallas_call(functools.partial(body, cfg), out_shape=pltpu.VMEM(spec_in...]
    unnamed x0 -> x1, local copies, waits for them, and re-layouts: none -> 0.72 us
where the time goes in v3:
time: 48.6 us; the launch traced here: 48.5 us
  Pallas kernels  47.8 us (98%)
  local copies, waits for them, and re-layouts  0.72 us (1%)
    pallas_call x1, Pallas kernels, block(): pl.pallas_call(functools.partial(body, cfg), out_shape=pltpu.VMEM(spec_in...  47.8 us

profile of v3, /device:TPU:1, one launch (start us, length us, event | category | flops | bytes accessed | tf_op | source)
XLA Modules:
  0.0 48.5 jit_solution(17150425881576559730)
XLA Ops:
  0.0 47.8 %spherical_block.1 = bf16[6,1,32,2,384]{4,3,2,1,0:T(2,128)(2,1)S(1)} custom-call(bf16[6,1,32,2,384]{4,3,2,1,0:T(2,128)(2,1)} %x_ref.1, f32[6,384,384]{2,1,0:T(8,128)} %leg_ref.1, bf16[2,384,768]{2,1,0:T(8,128)(2,1)} %constant.2.clone.table_ref, s32[384]{0:T(512)} %mode_hbm.1, bf16[512,256]{1,0:T(8,128)(2,1)} %w_in_ref.1, f32[1,512]{1,0:T(1,128)} %bitcast.3, ...), custom_call_target="tpu_custom_call" | custom-call | tf_op jit(solution)/shard_map/spherical_block/pallas_call | solution.py:484
  47.8 0.7 %copy.10 = bf16[6,1,32,2,384]{4,3,2,1,0:T(2,128)(2,1)} copy(bf16[6,1,32,2,384]{4,3,2,1,0:T(2,128)(2,1)S(1)} %spherical_block.1) | data formatting | bytes 589824

commit v4 on v3

--- a/solution.py
+++ b/solution.py
@@ -57,7 +57,7 @@
     rest = list(rest)
     take = lambda n: [rest.pop(0) for _ in range(n)]
     scr, s1, r1, lt, g, r2, mx, r3, s4, r4 = (take(nq) for _ in range(10))
-    leg_sem, in_sem, sends, recvs, locs = rest
+    in_sem, sends, recvs, locs = rest
 
     lat = lax.axis_index("lat")
     chan = lax.axis_index("chan")
@@ -67,10 +67,10 @@
     for q, nj in enumerate(chunks):
         rows_q = pl.ds(first_row[q], lat_n * nj)
         leg_copies.append(
-            [pltpu.make_async_copy(leg_ref.at[s, rows_q], legv.at[s, rows_q], leg_sem.at[q * slots + s]) for s in range(slots)]
+            [pltpu.make_async_copy(leg_ref.at[s, rows_q], legv.at[s, rows_q], locs.at[q]) for s in range(slots)]
         )
     in_copies = [
-        pltpu.make_async_copy(src, dst, in_sem.at[k])
+        pltpu.make_async_copy(src, dst, in_sem.at[k] if k < 5 else sends.at[nq + k - 5])
         for k, (src, dst) in enumerate(
             [(x_ref, xv), (mode_hbm, mode_ref), (table_ref, tab), (mode_hbm, mode_row), (w_in_ref, w_in), (b_ref, b_in), (w_out_ref, w_out), (kern_ref, kern)]
         )
@@ -110,21 +110,24 @@
     for copy in in_copies[3:]:
         copy.start()
 
+    def sent_sem(at):
+        return sends.at[at % nq if at // nq in (0, 3) else nq + at % nq]
+
     def start_lat(q, src, dst, at):
         def one(peer):
             pltpu.make_async_remote_copy(
-                src_ref=src.at[peer], dst_ref=dst.at[lat], send_sem=sends.at[at], recv_sem=recvs.at[at],
+                src_ref=src.at[peer], dst_ref=dst.at[lat], send_sem=sent_sem(at), recv_sem=recvs.at[at],
                 device_id={"lat": peer}, device_id_type=MESH,
             ).start()
 
         each_lat(one)
-        pltpu.make_async_copy(src.at[lat], dst.at[lat], locs.at[at]).start()
+        pltpu.make_async_copy(src.at[lat], dst.at[lat], locs.at[at % nq]).start()
 
     def wait_lat(q, src, dst, at):
-        pltpu.make_async_copy(src.at[lat], dst.at[lat], locs.at[at]).wait()
+        pltpu.make_async_copy(src.at[lat], dst.at[lat], locs.at[at % nq]).wait()
         pltpu.make_async_remote_copy(
             src_ref=src.at[pl.ds(0, lat_n - 1)], dst_ref=dst.at[pl.ds(0, lat_n - 1)],
-            send_sem=sends.at[at], recv_sem=recvs.at[at], device_id={"lat": (lat + 1) % lat_n}, device_id_type=MESH,
+            send_sem=sent_sem(at), recv_sem=recvs.at[at], device_id={"lat": (lat + 1) % lat_n}, device_id_type=MESH,
         ).wait()
 
     col_x = iota((cr, cr), 1)
@@ -156,8 +159,8 @@
     for q, nj in enumerate(chunks):
         span = slice(first_row[q], first_row[q] + lat_n * nj)
         degree = iota((lat_n * nj, deg), 1)
-        for copy in leg_copies[q]:
-            copy.wait()
+        rows_q = pl.ds(first_row[q], lat_n * nj)
+        pltpu.make_async_copy(leg_ref.at[:, rows_q], legv.at[:, rows_q], locs.at[q]).wait()
         masked = [jnp.where(degree >= modes_here[s], legv[s, span], 0.0).astype(BF16) for s in range(slots)]
         products = [dot(masked[s], spectra[s], NT) for s in range(slots)]
         for s in range(slots):
@@ -232,7 +235,7 @@
             for peer in chan_peers:
                 count = lambda size: act(
                     pltpu.make_async_remote_copy(
-                        src_ref=src_of(peer, size), dst_ref=dst_of(size), send_sem=sends.at[at],
+                        src_ref=src_of(peer, size), dst_ref=dst_of(size), send_sem=sent_sem(at),
                         recv_sem=recvs.at[at], device_id={"chan": peer}, device_id_type=MESH,
                     )
                 )
@@ -266,7 +269,7 @@
         def own(size):
             pltpu.make_async_copy(
                 g[q].at[pl.ds(chan * slots_of(q), size)],
-                r2[q].at[pl.ds(0, size), pl.ds(pl.multiple_of(chan * cl, cl), cl)], locs.at[at],
+                r2[q].at[pl.ds(0, size), pl.ds(pl.multiple_of(chan * cl, cl), cl)], locs.at[at % nq],
             ).start()
 
         by_size(q, own)
@@ -292,11 +295,11 @@
             span = (chan_n - 1) * cl
             pltpu.make_async_copy(
                 g[q].at[pl.ds(chan * slots_of(q), size)],
-                r2[q].at[pl.ds(0, size), pl.ds(pl.multiple_of(chan * cl, cl), cl)], locs.at[at],
+                r2[q].at[pl.ds(0, size), pl.ds(pl.multiple_of(chan * cl, cl), cl)], locs.at[at % nq],
             ).wait()
             pltpu.make_async_remote_copy(
                 src_ref=r2[q].at[pl.ds(0, size), pl.ds(0, span)], dst_ref=r2[q].at[pl.ds(0, size), pl.ds(0, span)],
-                send_sem=sends.at[at], recv_sem=recvs.at[at], device_id={"chan": (chan + 1) % chan_n}, device_id_type=MESH,
+                send_sem=sent_sem(at), recv_sem=recvs.at[at], device_id={"chan": (chan + 1) % chan_n}, device_id_type=MESH,
             ).wait_recv()
 
         by_size(q, act)
@@ -307,7 +310,7 @@
         def act(size):
             part = buffer.at[pl.ds(0, total - size)]
             pltpu.make_async_remote_copy(
-                src_ref=part, dst_ref=part, send_sem=sends.at[at], recv_sem=recvs.at[at],
+                src_ref=part, dst_ref=part, send_sem=sent_sem(at), recv_sem=recvs.at[at],
                 device_id={"chan": (chan + 1) % chan_n}, device_id_type=MESH,
             ).wait_send()
 
@@ -320,10 +323,10 @@
             for peer in chan_peers:
                 pltpu.make_async_remote_copy(
                     src_ref=mx[q].at[pl.ds(peer * slots_of(q), size)], dst_ref=r3[q].at[pl.ds(chan * slots_of(q), size)],
-                    send_sem=sends.at[at], recv_sem=recvs.at[at], device_id={"chan": peer}, device_id_type=MESH,
+                    send_sem=sent_sem(at), recv_sem=recvs.at[at], device_id={"chan": peer}, device_id_type=MESH,
                 ).start()
             pltpu.make_async_copy(
-                mx[q].at[pl.ds(chan * slots_of(q), size)], r3[q].at[pl.ds(chan * slots_of(q), size)], locs.at[at]
+                mx[q].at[pl.ds(chan * slots_of(q), size)], r3[q].at[pl.ds(chan * slots_of(q), size)], locs.at[at % nq]
             ).start()
 
         by_size(q, act)
@@ -334,27 +337,27 @@
 
         def act(size):
             pltpu.make_async_copy(
-                mx[q].at[pl.ds(chan * slots_of(q), size)], r3[q].at[pl.ds(chan * slots_of(q), size)], locs.at[at]
+                mx[q].at[pl.ds(chan * slots_of(q), size)], r3[q].at[pl.ds(chan * slots_of(q), size)], locs.at[at % nq]
             ).wait()
             peer = {"chan": (chan + 1) % chan_n}
             sent = mx[q].at[pl.ds(0, (chan_n - 1) * size)]
             pltpu.make_async_remote_copy(
-                src_ref=sent, dst_ref=sent, send_sem=sends.at[at], recv_sem=recvs.at[at], device_id=peer, device_id_type=MESH,
+                src_ref=sent, dst_ref=sent, send_sem=sent_sem(at), recv_sem=recvs.at[at], device_id=peer, device_id_type=MESH,
             ).wait_send()
             got = r3[q].at[pl.ds(0, total - size)]
             pltpu.make_async_remote_copy(
-                src_ref=got, dst_ref=got, send_sem=sends.at[at], recv_sem=recvs.at[at], device_id=peer, device_id_type=MESH,
+                src_ref=got, dst_ref=got, send_sem=sent_sem(at), recv_sem=recvs.at[at], device_id=peer, device_id_type=MESH,
             ).wait_recv()
 
         by_size(q, act)
 
     for q, nj in enumerate(chunks):
         wait_lat(q, s1[q], r1[q], q)
-        parts = unpack(q, r1[q])
+        parts = [part.astype(BF16) for part in unpack(q, r1[q])]
         for sr in range(2 * slots):
             lt[q][sr * lat_n : (sr + 1) * lat_n, :] = jnp.concatenate(
                 [part[:, cl * sr : cl * (sr + 1)] for part in parts], axis=1
-            ).astype(BF16)
+            )
         grid = dot(lt[q][...], wv[...], TN).astype(BF16)
         for jj in range(nj):
             for k in range(ptiles):
@@ -364,6 +367,7 @@
 
     for q, nj in enumerate(chunks):
         wait_points(q)
+        drain_sent(q, nq + q, g[q])
         for n in range(0, slots_of(q), 2):
             tiles = range(n, min(n + 2, slots_of(q)))
             points = jnp.concatenate([r2[q][tile] for tile in tiles], axis=1)
@@ -422,19 +426,18 @@
             field = jnp.concatenate([missing, field], axis=0)
             start -= edge
         span = slice(start, first_row[q] + n_rows)
-        for first in range(0, slots, pair):
-            left = dot(merge, field[:, first * cr : (first + pair) * cr], NT).astype(BF16)
-            for s in range(first, first + pair):
-                part = dot(left[(s - first) * cr : (s - first + 1) * cr], lb[s, span])
-                if q > 0:
-                    part = part + acc[s]
-                if q < nq - 1:
-                    acc[s] = part
-                else:
-                    out_ref[s, 0] = part.astype(BF16).reshape(cl, 2, deg)
-
-    for q in range(nq):
-        drain_sent(q, nq + q, g[q])
+        left = [
+            dot(merge, field[:, first * cr : (first + pair) * cr], NT).astype(BF16) for first in range(0, slots, pair)
+        ]
+        products = [
+            dot(left[s // pair][s % pair * cr : (s % pair + 1) * cr], lb[s, span]) for s in range(slots)
+        ]
+        for s in range(slots):
+            part = products[s] if q == 0 else products[s] + acc[s]
+            if q < nq - 1:
+                acc[s] = part
+            else:
+                out_ref[s, 0] = part.astype(BF16).reshape(cl, 2, deg)
 
 
 def block(cfg, table, spec_in, legendre, mode_slot, w_in, b_in, w_out, kernel):
@@ -475,11 +478,10 @@
     scratch += message() + message()
     nq = len(CHUNKS)
     scratch += [
-        pltpu.SemaphoreType.DMA((slots * nq,)),
-        pltpu.SemaphoreType.DMA((8,)),
+        pltpu.SemaphoreType.DMA((5,)),
+        pltpu.SemaphoreType.DMA((2 * nq,)),
         pltpu.SemaphoreType.DMA((4 * nq,)),
-        pltpu.SemaphoreType.DMA((4 * nq,)),
-        pltpu.SemaphoreType.DMA((4 * nq,)),
+        pltpu.SemaphoreType.DMA((nq,)),
     ]
     return pl.pallas_call(
         functools.partial(body, cfg),

time: 48.6 us -> 47.9 us (0.986)
  Pallas kernels: 47.8 us -> 47 us
    pallas_call x1, Pallas kernels: 47.8 us -> 47 us  [block(): pl.pallas_call(functools.partial(body, cfg), out_shape=pltpu.VMEM(spec_in...]
where the time goes in v4:
time: 47.9 us; the launch traced here: 47.8 us
  Pallas kernels  47 us (98%)
  local copies, waits for them, and re-layouts  0.72 us (2%)
    pallas_call x1, Pallas kernels, block(): pl.pallas_call(functools.partial(body, cfg), out_shape=pltpu.VMEM(spec_in...  47 us

profile of v4, /device:TPU:1, one launch (start us, length us, event | category | flops | bytes accessed | tf_op | source)
XLA Modules:
  0.0 47.8 jit_solution(16120957448046180616)
XLA Ops:
  0.0 47.0 %spherical_block.1 = bf16[6,1,32,2,384]{4,3,2,1,0:T(2,128)(2,1)S(1)} custom-call(bf16[6,1,32,2,384]{4,3,2,1,0:T(2,128)(2,1)} %x_ref.1, f32[6,384,384]{2,1,0:T(8,128)} %leg_ref.1, bf16[2,384,768]{2,1,0:T(8,128)(2,1)} %constant.2.clone.table_ref, s32[384]{0:T(512)} %mode_hbm.1, bf16[512,256]{1,0:T(8,128)(2,1)} %w_in_ref.1, f32[1,512]{1,0:T(1,128)} %bitcast.3, ...), custom_call_target="tpu_custom_call" | custom-call | tf_op jit(solution)/shard_map/spherical_block/pallas_call | solution.py:486
  47.0 0.7 %copy.10 = bf16[6,1,32,2,384]{4,3,2,1,0:T(2,128)(2,1)} copy(bf16[6,1,32,2,384]{4,3,2,1,0:T(2,128)(2,1)S(1)} %spherical_block.1) | data formatting | bytes 589824

commit v5 on v4

--- a/solution.py
+++ b/solution.py
@@ -22,6 +22,12 @@
 
 def dot(a, b, dims=NN, precision=None):
     return lax.dot_general(a, b, dims, preferred_element_type=F32, precision=precision)
+
+
+def gelu(x):
+    a = math.sqrt(2.0 / math.pi)
+    half = 0.5 * x
+    return half + half * jnp.tanh(x * (a + (a * 0.044715) * (x * x)))
 
 
 def far_first(k, size):
@@ -212,8 +218,18 @@
     def exact_chan(q):
         return chunks[q] * ptiles - (slots_of(q) - 1) * chan_n
 
+    def first_columns(q):
+        nj = chunks[q]
+        even = slots_of(q) == 2 and chan_n % nj == 0 and chan_n // nj < ptiles
+        return chan_n // nj if even else ptiles
+
     def place(q, tile):
-        n, at = tile // chan_n, tile % chan_n
+        head = first_columns(q)
+        if head < ptiles:
+            jj, k = tile // ptiles, tile % ptiles
+            n, at = (0, jj * head + k) if k < head else (1, jj * (ptiles - head) + k - head)
+        else:
+            n, at = tile // chan_n, tile % chan_n
         if n == slots_of(q) - 1 and 2 * exact_chan(q) == chan_n:
             at = 2 * at + q % 2
         return at, n
@@ -227,49 +243,27 @@
         at, n = place(q, tile)
         return at * slots_of(q) + n
 
-    def chan_copies(q, src_of, dst_of, at):
-        n = slots_of(q)
-        even = exact_chan(q) == chan_n
-
-        def run(act):
-            for peer in chan_peers:
-                count = lambda size: act(
-                    pltpu.make_async_remote_copy(
-                        src_ref=src_of(peer, size), dst_ref=dst_of(size), send_sem=sent_sem(at),
-                        recv_sem=recvs.at[at], device_id={"chan": peer}, device_id_type=MESH,
-                    )
-                )
-                if even:
-                    count(n)
-                else:
-                    full = is_full(q, peer)
-
-                    @pl.when(full)
-                    def _():
-                        count(n)
-
-                    @pl.when(jnp.logical_not(full))
-                    def _():
-                        count(n - 1)
-
-        return run
-
-    def grid_src(q):
-        return lambda peer, size: g[q].at[pl.ds(peer * slots_of(q), size)]
-
-    def start_points(q):
+    def start_points(q, n):
         at = nq + q
-        chan_copies(
-            q, grid_src(q),
-            lambda size: r2[q].at[pl.ds(0, size), pl.ds(pl.multiple_of(chan * cl, cl), cl)],
-            at,
-        )(lambda copy: copy.start())
-        n = slots_of(q)
-
+        columns = pl.ds(pl.multiple_of(chan * cl, cl), cl)
+
+        def send(peer):
+            pltpu.make_async_remote_copy(
+                src_ref=g[q].at[peer * slots_of(q) + n], dst_ref=r2[q].at[n, columns], send_sem=sent_sem(at),
+                recv_sem=recvs.at[at], device_id={"chan": peer}, device_id_type=MESH,
+            ).start()
+
+        for peer in chan_peers:
+            if n < slots_of(q) - 1 or exact_chan(q) == chan_n:
+                send(peer)
+            else:
+                pl.when(is_full(q, peer))(functools.partial(send, peer))
+
+    def start_own(q):
         def own(size):
             pltpu.make_async_copy(
                 g[q].at[pl.ds(chan * slots_of(q), size)],
-                r2[q].at[pl.ds(0, size), pl.ds(pl.multiple_of(chan * cl, cl), cl)], locs.at[at % nq],
+                r2[q].at[pl.ds(0, size), pl.ds(pl.multiple_of(chan * cl, cl), cl)], locs.at[q],
             ).start()
 
         by_size(q, own)
@@ -358,12 +352,22 @@
             lt[q][sr * lat_n : (sr + 1) * lat_n, :] = jnp.concatenate(
                 [part[:, cl * sr : cl * (sr + 1)] for part in parts], axis=1
             )
-        grid = dot(lt[q][...], wv[...], TN).astype(BF16)
-        for jj in range(nj):
-            for k in range(ptiles):
-                tile = jj * ptiles + k
-                g[q][flat(q, tile)] = grid[cl * jj : cl * (jj + 1), 128 * k : 128 * (k + 1)]
-        start_points(q)
+        head = first_columns(q)
+        turned = lt[q][...].T
+        for low, high in ((0, head), (head, ptiles)):
+            if low == high:
+                continue
+            grid = dot(turned, wv[:, 128 * low : 128 * high]).astype(BF16)
+            for jj in range(nj):
+                for k in range(low, high):
+                    part = grid[cl * jj : cl * (jj + 1), 128 * (k - low) : 128 * (k - low + 1)]
+                    g[q][flat(q, jj * ptiles + k)] = part
+            if head < ptiles:
+                start_points(q, 0 if low == 0 else 1)
+        if head == ptiles:
+            for n in range(slots_of(q)):
+                start_points(q, n)
+        start_own(q)
 
     for q, nj in enumerate(chunks):
         wait_points(q)
@@ -372,7 +376,7 @@
             tiles = range(n, min(n + 2, slots_of(q)))
             points = jnp.concatenate([r2[q][tile] for tile in tiles], axis=1)
             pre = dot(w_in[...], points)
-            hidden = jax.nn.gelu(pre + jnp.concatenate([bias for _ in tiles], axis=1), approximate=True).astype(BF16)
+            hidden = gelu(pre + jnp.concatenate([bias for _ in tiles], axis=1)).astype(BF16)
             mixed = (points.astype(F32) + dot(w_out[...], hidden)).astype(BF16)
             for dest in range(chan_n):
                 for k, tile in enumerate(tiles):
@@ -387,11 +391,12 @@
         for jj in range(nj):
             tiles = [jj * ptiles + k for k in range(ptiles)]
             field.append(jnp.concatenate([r3[q][flat(q, tile)] for tile in tiles], axis=1))
-        modes = dot(jnp.concatenate(field, axis=0), wvt[...]).T
+        modes = dot(jnp.concatenate(field, axis=0), wvt[...]).astype(BF16).T
         for jj in range(nj):
             value = jnp.concatenate(
                 [modes[lat_n * sr : lat_n * (sr + 1), cl * jj : cl * (jj + 1)] for sr in range(2 * slots)], axis=1
             )
+            value = value.astype(F32)
             for k in range(ltiles):
                 scr[q][k, pl.ds(jj, lat_n, stride=nj), :] = value[:, 128 * k : 128 * (k + 1)]
         s4[q][...] = message(q)

time: 47.9 us -> 47.7 us (level)
  no operation moved by 1% of the time
where the time goes in v5:
time: 47.7 us; the launch traced here: 47.6 us
  Pallas kernels  46.9 us (98%)
  local copies, waits for them, and re-layouts  0.72 us (2%)
    pallas_call x1, Pallas kernels, block(): pl.pallas_call(functools.partial(body, cfg), out_shape=pltpu.VMEM(spec_in...  46.9 us

profile of v5, /device:TPU:1, one launch (start us, length us, event | category | flops | bytes accessed | tf_op | source)
XLA Modules:
  0.0 47.6 jit_solution(5373250277725546629)
XLA Ops:
  0.0 46.9 %spherical_block.1 = bf16[6,1,32,2,384]{4,3,2,1,0:T(2,128)(2,1)S(1)} custom-call(bf16[6,1,32,2,384]{4,3,2,1,0:T(2,128)(2,1)} %x_ref.1, f32[6,384,384]{2,1,0:T(8,128)} %leg_ref.1, bf16[2,384,768]{2,1,0:T(8,128)(2,1)} %constant.2.clone.table_ref, s32[384]{0:T(512)} %mode_hbm.1, bf16[512,256]{1,0:T(8,128)(2,1)} %w_in_ref.1, f32[1,512]{1,0:T(1,128)} %bitcast.3, ...), custom_call_target="tpu_custom_call" | custom-call | tf_op jit(solution)/shard_map/spherical_block/pallas_call | solution.py:491
  46.9 0.7 %copy.10 = bf16[6,1,32,2,384]{4,3,2,1,0:T(2,128)(2,1)} copy(bf16[6,1,32,2,384]{4,3,2,1,0:T(2,128)(2,1)S(1)} %spherical_block.1) | data formatting | bytes 589824

commit v6 on v5

--- a/solution.py
+++ b/solution.py
@@ -85,21 +85,17 @@
 
     nx, nz, nc = grid3
     here_x, here_z, here_c = lat // (nz * nc), (lat // nc) % nz, lat % nc
-    peer_x = [((here_x + far_first(k, nx)) % nx) * (nz * nc) for k in range(nx)]
-    peer_c = [(here_c + nc - 1 - k) % nc for k in range(nc)]
-    peer_xc = [x + c for x in peer_x for c in peer_c]
+    peer_x = [((here_x + dx) % nx) * (nz * nc) for dx in range(nx)]
+    peer_z = [((here_z + dz) % nz) * nc for dz in range(nz)]
+    peer_c = [(here_c + dc) % nc for dc in range(nc)]
+    steps = [(dx, dz, dc) for dx in range(nx) for dz in range(nz) for dc in range(nc)]
+    steps.sort(key=lambda step: -min(step[0], nx - step[0]) - min(step[1], nz - step[1]))
+    steps.remove((0, 0, 0))
     chan_peers = [(chan + far_first(k, chan_n)) % chan_n for k in range(chan_n - 1)]
 
     def each_lat(act):
-        def at_z(k, carry):
-            z = ((here_z + far_first(k, nz)) % nz) * nc
-            for base in peer_xc:
-                act(base + z)
-            return carry
-
-        lax.fori_loop(0, nz - 1, at_z, 0)
-        for base in peer_xc[:-1]:
-            act(base + here_z * nc)
+        for dx, dz, dc in steps:
+            act(peer_x[dx] + peer_z[dz] + peer_c[dc])
 
     in_copies[0].start()
     in_copies[1].start()

time: 47.7 us -> 47.9 us (level)
  no operation moved by 1% of the time
where the time goes in v6:
time: 47.9 us; the launch traced here: 47.8 us
  Pallas kernels  47.1 us (98%)
  local copies, waits for them, and re-layouts  0.72 us (2%)
    pallas_call x1, Pallas kernels, block(): pl.pallas_call(functools.partial(body, cfg), out_shape=pltpu.VMEM(spec_in...  47.1 us

profile of v6, /device:TPU:1, one launch (start us, length us, event | category | flops | bytes accessed | tf_op | source)
XLA Modules:
  0.0 47.8 jit_solution(6244413629793941497)
XLA Ops:
  0.0 47.1 %spherical_block.1 = bf16[6,1,32,2,384]{4,3,2,1,0:T(2,128)(2,1)S(1)} custom-call(bf16[6,1,32,2,384]{4,3,2,1,0:T(2,128)(2,1)} %x_ref.1, f32[6,384,384]{2,1,0:T(8,128)} %leg_ref.1, bf16[2,384,768]{2,1,0:T(8,128)(2,1)} %constant.2.clone.table_ref, s32[384]{0:T(512)} %mode_hbm.1, bf16[512,256]{1,0:T(8,128)(2,1)} %w_in_ref.1, f32[1,512]{1,0:T(1,128)} %bitcast.3, ...), custom_call_target="tpu_custom_call" | custom-call | tf_op jit(solution)/shard_map/spherical_block/pallas_call | solution.py:487
  47.1 0.7 %copy.10 = bf16[6,1,32,2,384]{4,3,2,1,0:T(2,128)(2,1)} copy(bf16[6,1,32,2,384]{4,3,2,1,0:T(2,128)(2,1)S(1)} %spherical_block.1) | data formatting | bytes 589824

commit v7 on v4

--- a/solution.py
+++ b/solution.py
@@ -95,14 +95,13 @@
         for base in peer_xc[:-1]:
             act(base + here_z * nc)
 
+    each_lat(lambda peer: pl.semaphore_signal(barrier, inc=1, device_id={"lat": peer}, device_id_type=MESH))
+    for peer in chan_peers:
+        pl.semaphore_signal(barrier, inc=1, device_id={"chan": peer}, device_id_type=MESH)
     in_copies[0].start()
     in_copies[1].start()
     for copy in leg_copies[0]:
         copy.start()
-
-    each_lat(lambda peer: pl.semaphore_signal(barrier, inc=1, device_id={"lat": peer}, device_id_type=MESH))
-    for peer in chan_peers:
-        pl.semaphore_signal(barrier, inc=1, device_id={"chan": peer}, device_id_type=MESH)
     in_copies[2].start()
     for per in leg_copies[1:]:
         for copy in per:

time: 47.9 us -> 47.9 us (level)
  no operation moved by 1% of the time
where the time goes in v7:
time: 47.9 us; the launch traced here: 47.8 us
  Pallas kernels  47.1 us (98%)
  local copies, waits for them, and re-layouts  0.72 us (2%)
    pallas_call x1, Pallas kernels, block(): pl.pallas_call(functools.partial(body, cfg), out_shape=pltpu.VMEM(spec_in...  47.1 us

profile of v7, /device:TPU:1, one launch (start us, length us, event | category | flops | bytes accessed | tf_op | source)
XLA Modules:
  0.0 47.8 jit_solution(3904421495980379236)
XLA Ops:
  0.0 47.1 %spherical_block.1 = bf16[6,1,32,2,384]{4,3,2,1,0:T(2,128)(2,1)S(1)} custom-call(bf16[6,1,32,2,384]{4,3,2,1,0:T(2,128)(2,1)} %x_ref.1, f32[6,384,384]{2,1,0:T(8,128)} %leg_ref.1, bf16[2,384,768]{2,1,0:T(8,128)(2,1)} %constant.2.clone.table_ref, s32[384]{0:T(512)} %mode_hbm.1, bf16[512,256]{1,0:T(8,128)(2,1)} %w_in_ref.1, f32[1,512]{1,0:T(1,128)} %bitcast.3, ...), custom_call_target="tpu_custom_call" | custom-call | tf_op jit(solution)/shard_map/spherical_block/pallas_call | solution.py:485
  47.1 0.7 %copy.10 = bf16[6,1,32,2,384]{4,3,2,1,0:T(2,128)(2,1)} copy(bf16[6,1,32,2,384]{4,3,2,1,0:T(2,128)(2,1)S(1)} %spherical_block.1) | data formatting | bytes 589824
